TPU v7x, 32 devices: a whole 2x2x4 slice. The times are simulated.
32 devices in a mesh: scan: 16 (over z, x, core), tile: 2 (over y).
Axes of the slice: x: 2, y: 2, z: 4, core: 2. Of those that a mesh axis runs over, the one named last changes fastest.
Arguments:
- probe_modes: float32 [12, 2, 128, 128], replicated, may hold values from -5 to 5
- patterns: float32 [128, 128, 128], P(('scan', 'tile')), may hold values from 0.005 to 300
- specimen: float32 [2, 2048, 512], P(None, 'scan', 'tile'), may hold values from -17.5 to 17.5
- offsets: int32 [128, 2], P(('scan', 'tile')), may hold values from -128 to 2048, as said below
Outputs:
- new_probe: float32 [12, 2, 128, 128], replicated
- new_specimen: float32 [2, 2048, 512], P(None, 'scan', 'tile')
Inputs may be any that keep to these rules, and one draw needn't show every extreme that they name: `offsets`: position p lies in aligned block b = p // 4, held by the device of scan index s = b // (the number of tile devices) and tile index t = b % (the number of tile devices); its row offset lies in s * 128 - 128 to s * 128 + 128, its column offset in t * 256 - 128 to t * 256 + 256, both ends included; in every block one position has its row offset at the lower end and its column offset at the upper end, and one has its row offset at the upper end.
All inputs are finite; a program needn't handle non-finite values.
Results may differ from a plain program's by a relative error of at most 0.0001.
Values sent between devices are 32-bit elements; how exact they have to be, the bound alone decides.
No kernel may reach another device: no remote copies, remote signals or barrier semaphores. Data moves between devices by JAX's collectives and lax.ppermute only.
A program may use at most 64 MiB of HBM per device.

v0:
```python
import math

import jax
import jax.numpy as jnp
import numpy as np
from jax import lax
from jax.experimental import pallas as pl
from jax.experimental.pallas import tpu as pltpu
from jax.sharding import PartitionSpec as P


NS_STEPS = 8
AXES = ("scan", "tile")
light_floor = 0.05
object_reg = 0.5
probe_reg = 1.0
total_eps = 1e-06
f32 = jnp.float32
bf16 = jnp.bfloat16
highest = lax.Precision.HIGHEST


def dft_tables(detector):
    index = np.arange(detector, dtype=np.int64)
    angle = -2.0 * np.pi / detector * (index[:, None] * index[None, :] % detector)
    cos = np.cos(angle) / math.sqrt(detector)
    sin = np.sin(angle) / math.sqrt(detector)
    first = np.block([[cos, sin], [-sin, cos]]).astype(np.float32)
    second = np.block([[cos, -sin], [sin, cos]]).astype(np.float32)
    tables = []
    for table in (first, second):
        high = table.astype(bf16)
        low = (table - high.astype(np.float32)).astype(bf16)
        tables.append((high, low))
    (fh, fl), (sh, sl) = tables
    right_fwd = np.concatenate([fh, fh, fl], axis=0)
    right_inv = np.concatenate([sh, sh, sl], axis=0)
    left_fwd = np.concatenate([sh, sh, sl], axis=1)
    left_inv = np.concatenate([fh, fh, fl], axis=1)
    return tuple(jnp.asarray(t) for t in (right_fwd, left_fwd, right_inv, left_inv))


def split(values):
    high = values.astype(bf16)
    low = (values - high.astype(f32)).astype(bf16)
    return high, low


def right_product(rows, table):
    high, low = split(rows)
    return jnp.dot(jnp.concatenate([high, low, high], axis=1), table, preferred_element_type=f32)


def left_product(table, columns):
    high, low = split(columns)
    return jnp.dot(table, jnp.concatenate([high, low, high], axis=0), preferred_element_type=f32)


def to_columns(rows, n):
    top = jnp.concatenate([rows[:n, :n], rows[n:, :n]], axis=1)
    bottom = jnp.concatenate([rows[:n, n:], rows[n:, n:]], axis=1)
    return jnp.concatenate([top, bottom], axis=0)


def prepare_kernel(*refs):
    inputs, outputs, power, root, measured, done = refs[:7], refs[7:14], *refs[14:]
    copies = [
        pltpu.make_async_copy(src, dst, done.at[i])
        for i, (src, dst) in enumerate(zip(inputs, outputs))
    ]
    for copy in copies:
        copy.start()
    for copy in copies[:2]:
        copy.wait()
    probe, patterns = outputs[:2]
    modes, _, n, _ = probe.shape
    total = jnp.zeros((n, n), f32)
    for k in range(modes):
        total = total + probe[k, 0] * probe[k, 0] + probe[k, 1] * probe[k, 1]
    power[...] = total
    light = jnp.zeros((8, n), f32)
    for p in range(patterns.shape[0]):
        values = patterns[p]
        root[p] = jnp.sqrt(values)
        light = light + jnp.sum(values.reshape(n // 8, 8, n), axis=0)
    measured[...] = light
    for copy in copies[2:]:
        copy.wait()


def positions_kernel(
    where, probe, root, power, measured, own, side_a, side_b, strip_y, strip_a, strip_b,
    right_fwd, left_fwd, right_inv, left_inv,
    *refs,
):
    parts = refs[: 2 * PARTS]
    fold_own, fold_a, fold_b, fold_y, fold_ya, fold_yb = refs[2 * PARTS : 2 * PARTS + 6]
    sums, extended, frame, far, patch, model, numer = refs[2 * PARTS + 6 :]
    modes, _, n, _ = probe.shape
    count = root.shape[0]
    rows, cols = own.shape[1:]
    even = where[2 * count] == 0
    first_tile = where[2 * count + 1] == 0
    row_a = pl.multiple_of(jnp.where(even, n + rows, 0), n)
    row_b = pl.multiple_of(jnp.where(even, 0, n + rows), n)
    col_y = pl.multiple_of(jnp.where(first_tile, n + cols, 0), n)
    col_z = pl.multiple_of(jnp.where(first_tile, 0, n + cols), n)

    frame[...] = jnp.zeros_like(frame)
    extended[:, :, pl.ds(col_z, n)] = jnp.zeros((2, extended.shape[1], n), f32)
    extended[:, n : n + rows, n : n + cols] = own[...]
    extended[:, pl.ds(row_a, n), n : n + cols] = side_a[...]
    extended[:, pl.ds(row_b, n), n : n + cols] = side_b[...]
    extended[:, n : n + rows, pl.ds(col_y, n)] = strip_y[...]
    extended[:, pl.ds(row_a, n), pl.ds(col_y, n)] = strip_a[...]
    extended[:, pl.ds(row_b, n), pl.ds(col_y, n)] = strip_b[...]

    sums[...] = jnp.zeros_like(sums)
    sums[2 * modes + 1, 8:16] = measured[...]
    pairs = modes // 2

    def one_position(p, carry):
        row = where[p]
        col = where[count + p]
        col_block = pl.multiple_of(col // n * n, n)
        shift = col - col_block
        row_block = pl.multiple_of(row // 8 * 8, 8)
        down = row - row_block
        for c in range(2):
            window = extended[c, pl.ds(row_block, n + 8), pl.ds(col_block, 2 * n)]
            window = pltpu.roll(window, (2 * n - shift) % (2 * n), 1)[:, :n]
            patch[c] = pltpu.roll(window, (n + 8 - down) % (n + 8), 0)[:n]
        model[...] = jnp.zeros_like(model)

        def forward(q, carry):
            p_re = patch[0]
            p_im = patch[1]
            blocks = []
            for k in range(2):
                re = probe[2 * q + k, 0]
                im = probe[2 * q + k, 1]
                blocks.append(
                    jnp.concatenate([re * p_re - im * p_im, re * p_im + im * p_re], axis=1)
                )
            half = right_product(jnp.concatenate(blocks, axis=0), right_fwd[...])
            full = left_product(left_fwd[...], to_columns(half, n))
            far[q] = full
            squares = full * full
            squares = squares[:n] + squares[n:]
            model[...] += squares[:, :n] + squares[:, n:]
            return carry

        lax.fori_loop(0, pairs, forward, 0, unroll=UNROLL)
        light = model[...]
        factor = root[p] / jnp.sqrt(jnp.maximum(light, light_floor)) - 1.0
        model[...] = factor
        sums[2 * modes + 1, 0:8] += jnp.sum(light.reshape(n // 8, 8, n), axis=0)
        numer[...] = jnp.zeros_like(numer)

        def backward(q, carry):
            factor = model[...]
            factor4 = jnp.concatenate([factor, factor], axis=1)
            factor4 = jnp.concatenate([factor4, factor4], axis=0)
            half = right_product(to_columns(far[q] * factor4, n), right_inv[...])
            change = left_product(left_inv[...], to_columns(half, n))
            p_re = patch[0]
            p_im = patch[1]
            num_re = numer[0]
            num_im = numer[1]
            for k in range(2):
                c_re = change[:n, k * n : (k + 1) * n]
                c_im = change[n:, k * n : (k + 1) * n]
                re = probe[2 * q + k, 0]
                im = probe[2 * q + k, 1]
                at = 4 * q + 2 * k
                sums[at] += p_re * c_re + p_im * c_im
                sums[at + 1] += p_re * c_im - p_im * c_re
                num_re = num_re + (re * c_re + im * c_im)
                num_im = num_im + (re * c_im - im * c_re)
            numer[0] = num_re
            numer[1] = num_im
            return carry

        lax.fori_loop(0, pairs, backward, 0, unroll=UNROLL)
        sums[2 * modes] += patch[0] * patch[0] + patch[1] * patch[1]
        for c in range(3):
            value = power[...] if c == 2 else numer[c]
            tall = pltpu.roll(jnp.concatenate([value, jnp.zeros((8, n), f32)], axis=0), down, 0)
            wide = pltpu.roll(jnp.concatenate([tall, jnp.zeros_like(tall)], axis=1), shift, 1)
            frame[c, pl.ds(row_block, n + 8), pl.ds(col_block, 2 * n)] += wide
        return carry

    lax.fori_loop(0, count, one_position, 0)
    half_rows = n // 2
    core = where[2 * count]
    mine = pl.multiple_of(core * half_rows, half_rows)
    theirs = pl.multiple_of((1 - core) * half_rows, half_rows)
    for h, (keep, send) in enumerate(zip(parts[0::2], parts[1::2])):
        planes = keep.shape[0]
        keep[...] = sums[h * planes : (h + 1) * planes, pl.ds(mine, half_rows)]
        send[...] = sums[h * planes : (h + 1) * planes, pl.ds(theirs, half_rows)]
    fold_own[...] = frame[:, n : n + rows, n : n + cols]
    fold_a[...] = frame[:, pl.ds(row_a, n), n : n + cols]
    fold_b[...] = frame[:, pl.ds(row_b, n), n : n + cols]
    fold_y[...] = frame[:, n : n + rows, pl.ds(col_y, n)]
    fold_ya[...] = frame[:, pl.ds(row_a, n), pl.ds(col_y, n)]
    fold_yb[...] = frame[:, pl.ds(row_b, n), pl.ds(col_y, n)]


UNROLL = 6
PARTS = 2


def object_kernel(where, specimen, own, side_a, side_b, strip_y, strip_a, strip_b, out):
    n = strip_y.shape[2]
    cols = own.shape[2]
    first_tile = where[where.shape[0] - 2] == 0
    at = pl.multiple_of(jnp.where(first_tile, cols - n, 0), n)
    own[...] += side_a[...] + side_b[...]
    own[:, :, pl.ds(at, n)] += strip_y[...] + strip_a[...] + strip_b[...]
    light = own[2] + object_reg
    out[0] = specimen[0] + own[0] / light
    out[1] = specimen[1] + own[1] / light


def split_kernel(where, keep, received, *outs):
    quarter = where[where.shape[0] - 1]
    rows = outs[0].shape[1]
    for k, out in enumerate(outs):
        at = pl.ds(pl.multiple_of((quarter ^ k) * rows, rows), rows)
        out[...] = keep[:, at] + received[:, at]


def join_kernel(where, *refs):
    quarter = where[where.shape[0] - 1]
    out = refs[-1]
    rows = refs[0].shape[1]
    for k, ref in enumerate(refs[:-1]):
        out[:, pl.ds(pl.multiple_of((quarter ^ k) * rows, rows), rows)] = ref[...]


def probe_kernel(where, probe, *refs):
    parts = refs[: 2 * PARTS]
    out, updated, sums, result, wide, done = refs[2 * PARTS :]
    modes, _, n, _ = probe.shape
    planes = 2 * modes
    half_rows = n // 2
    core = where[where.shape[0] - 3]
    mine = pl.multiple_of(core * half_rows, half_rows)
    theirs = pl.multiple_of((1 - core) * half_rows, half_rows)
    for h, (own, mate) in enumerate(zip(parts[0::2], parts[1::2])):
        part = own.shape[0]
        sums[h * part : (h + 1) * part, pl.ds(mine, half_rows)] = own[...]
        sums[h * part : (h + 1) * part, pl.ds(theirs, half_rows)] = mate[...]
    scale = 1.0 / (sums[planes] + probe_reg)

    def update(k, carry):
        for c in range(2):
            updated[2 * k + c] = probe[k, c] + sums[2 * k + c] * scale
        return carry

    lax.fori_loop(0, modes, update, 0)
    for k in range(planes, updated.shape[0]):
        updated[k] = jnp.zeros((n, n), f32)
    model_all = jnp.sum(sums[planes + 1, 0:8], keepdims=True)
    measured_all = jnp.sum(sums[planes + 1, 8:16], keepdims=True)
    ratio = measured_all / (model_all + total_eps)

    def rows_of(x, count):
        blocks = [
            updated[0:count, pl.ds(pl.multiple_of(x + i, 8), 8), :].reshape(8 * count, n)
            for i in (0, 8)
        ]
        return jnp.concatenate(blocks, axis=1)

    def mul(a, b):
        return jnp.dot(a, b, precision=highest, preferred_element_type=f32)

    tall = 8 * planes
    wide[...] = jnp.zeros_like(wide)

    def accumulate(b, carry):
        left, right = [], []
        for x in (0, 16):
            high, low = split(rows_of(32 * b + x, planes))
            left += [high, low, high, low]
            right += [high, high, low, low]
        wide[...] += lax.dot_general(
            jnp.concatenate(left, axis=1),
            jnp.concatenate(right, axis=1),
            (((1,), (1,)), ((), ())),
            preferred_element_type=f32,
        )
        return carry

    lax.fori_loop(0, n // 32, accumulate, 0, unroll=4)
    wide_gram = wide[...]
    r0 = lax.broadcasted_iota(jnp.int32, (tall, tall), 0)
    r1 = lax.broadcasted_iota(jnp.int32, (tall, tall), 1)
    same_row = r0 % 8 == r1 % 8
    spread = jnp.where(
        lax.broadcasted_iota(jnp.int32, (tall, planes), 0) // 8
        == lax.broadcasted_iota(jnp.int32, (tall, planes), 1),
        1.0,
        0.0,
    )
    gather = jnp.where(
        lax.broadcasted_iota(jnp.int32, (planes, tall), 1) // 8
        == lax.broadcasted_iota(jnp.int32, (planes, tall), 0),
        1.0,
        0.0,
    )
    i0 = lax.broadcasted_iota(jnp.int32, (planes, planes), 0)
    i1 = lax.broadcasted_iota(jnp.int32, (planes, planes), 1)
    identity = jnp.where(i0 == i1, 1.0, 0.0)

    def turned(lead, follow):
        up = jnp.where(lead == follow + 1, jnp.where(follow % 2 == 0, 1.0, 0.0), 0.0)
        return up - jnp.where(follow == lead + 1, jnp.where(lead % 2 == 0, 1.0, 0.0), 0.0)

    spread_turned = turned(
        lax.broadcasted_iota(jnp.int32, (tall, planes), 0) // 8,
        lax.broadcasted_iota(jnp.int32, (tall, planes), 1),
    )
    gather_turned = turned(
        lax.broadcasted_iota(jnp.int32, (planes, tall), 0),
        lax.broadcasted_iota(jnp.int32, (planes, tall), 1) // 8,
    )
    wide_gram = jnp.where(same_row, wide_gram, 0.0)
    hermitian = mul(gather, mul(wide_gram, spread)) - mul(
        gather_turned, mul(wide_gram, spread_turned)
    )
    frobenius = jnp.sqrt(jnp.sum(hermitian * hermitian, keepdims=True))

    def newton(_, carry):
        current, inverse = carry
        factor = 1.5 * identity - 0.5 * mul(inverse, current)
        return mul(current, factor), mul(factor, inverse)

    _, inverse = lax.fori_loop(0, NS_STEPS, newton, (hermitian / frobenius, identity))
    inverse = inverse / jnp.sqrt(frobenius)
    diagonal = jnp.sum(hermitian * identity, axis=1, keepdims=True)
    mix = inverse * jnp.sqrt(ratio * diagonal)
    full = 8 * updated.shape[0]

    def rows8(values):
        return jnp.broadcast_to(values[:, None, :], (planes, 8, tall)).reshape(tall, tall)

    wide_mix = jnp.where(same_row, rows8(mul(mix, gather)), 0.0)
    wide_mix = jnp.concatenate([wide_mix, jnp.zeros((tall, full - tall), f32)], axis=1)
    high, low = split(wide_mix)
    table = jnp.concatenate([high, high, low], axis=1)

    def out_copy(b):
        at = pl.ds(pl.multiple_of(32 * b, 32), 32)
        return pltpu.make_async_copy(result.at[:, at, :], out.at[:, at, :], done.at[b])

    def orthogonalize(b, carry):
        for x in (0, 16):
            mixed = left_product(table, rows_of(32 * b + x, updated.shape[0]))
            for i in range(2):
                at = pl.ds(pl.multiple_of(32 * b + x + 8 * i, 8), 8)
                result[:, at, :] = mixed[:, i * n : (i + 1) * n].reshape(planes, 8, n)
        out_copy(b).start()
        return carry

    lax.fori_loop(0, n // 32, orthogonalize, 0, unroll=4)

    def drain(b, carry):
        out_copy(b).wait()
        return carry

    lax.fori_loop(0, n // 32, drain, 0)


def vmem(count):
    return [pl.BlockSpec(memory_space=pltpu.VMEM)] * count


def on_chip(*arrays):
    return tuple(pltpu.with_memory_space_constraint(a, pltpu.VMEM) for a in arrays)


def limit(mib):
    return pltpu.CompilerParams(vmem_limit_bytes=mib * 2**20)


def partners(scan, tile):
    def flat(s, t):
        return s * tile + t

    mates, others, across, mates_across, others_across = [], [], [], [], []
    for s in range(scan):
        mate = s ^ 1
        other = s + 1 if s % 2 else s - 1
        for t in range(tile):
            here = flat(s, t)
            mates.append((here, flat(mate, t)))
            across.append((here, flat(s, 1 - t)))
            mates_across.append((here, flat(mate, 1 - t)))
            if 0 <= other < scan:
                others.append((here, flat(other, t)))
                others_across.append((here, flat(other, 1 - t)))
    return mates, others, across, mates_across, others_across


def send(array, pairs):
    return lax.ppermute(array, AXES, pairs)


def peers(scan, tile, scan_flip, tile_flip):
    return [
        (s * tile + t, (s ^ scan_flip) * tile + (t ^ tile_flip))
        for s in range(scan)
        for t in range(tile)
    ]


def probe_update(where, probe_chip, keeps, sends, mates, scan, tile):
    modes, _, n, _ = probe_chip.shape
    group = [peers(scan, tile, 2 * (k // 2), k % 2) for k in range(1, 4)]
    smem = pl.BlockSpec(memory_space=pltpu.SMEM)
    joined = []
    for keep, other in zip(keeps, sends):
        planes, rows, _ = keep.shape
        received = send(other, mates)
        block = pltpu.VMEM((planes, rows // 4, n), f32)
        own, *others = pl.pallas_call(
            split_kernel,
            out_shape=(block,) * 4,
            in_specs=[smem] + vmem(2),
            out_specs=tuple(vmem(4)),
            name="split",
        compiler_params=limit(4),
        )(where, *on_chip(keep, received))
        total = own
        arrived = [send(other, perm) for other, perm in zip(others, group)]
        total = own + arrived[0] + arrived[1] + arrived[2]
        flip = 4
        while flip < scan:
            total = total + send(total, peers(scan, tile, 2 * flip - 4, 0))
            flip = flip * 2
        arrived = [send(total, perm) for perm in group]
        mine = pl.pallas_call(
            join_kernel,
            out_shape=pltpu.VMEM(keep.shape, f32),
            in_specs=[smem] + vmem(4),
            out_specs=vmem(1)[0],
            name="join",
        compiler_params=limit(4),
        )(where, *on_chip(total, *arrived))
        joined += [mine, send(mine, mates)]
    planes = 2 * modes
    return pl.pallas_call(
        probe_kernel,
        out_shape=jax.ShapeDtypeStruct((planes, n, n), f32),
        in_specs=[smem] + vmem(1 + 2 * PARTS),
        out_specs=pl.BlockSpec(memory_space=pl.ANY),
        scratch_shapes=[
            pltpu.VMEM((-(-planes // 32) * 32, n, n), f32),
            pltpu.VMEM((planes + 2, n, n), f32),
            pltpu.VMEM((planes, n, n), f32),
            pltpu.VMEM((8 * planes, 8 * planes), f32),
            pltpu.SemaphoreType.DMA((n // 32,)),
        ],
        name="probe",
        compiler_params=limit(20),
    )(where, *on_chip(probe_chip, *joined))


def program(probe_modes, patterns, specimen, offsets):
    modes, _, n, _ = probe_modes.shape
    count = patterns.shape[0]
    rows, cols = specimen.shape[1:]
    scan = lax.axis_size("scan")
    tile = lax.axis_size("tile")
    assert tile == 2 and scan >= 4 and scan & (scan - 1) == 0 and rows == n and modes % 2 == 0
    s = lax.axis_index("scan")
    t = lax.axis_index("tile")
    where = jnp.concatenate(
        [
            offsets[:, 0] - (s * rows - n),
            offsets[:, 1] - (t * cols - n),
            jnp.stack([s % 2, t, s // 2 % 2 * 2 + t]).astype(jnp.int32),
        ]
    )
    pairs = partners(scan, tile)
    strip = lax.dynamic_slice(specimen, (0, 0, (1 - t) * (cols - n)), (2, rows, n))
    side_b = send(specimen, pairs[1])
    strip_b = send(strip, pairs[4])
    strip_y = send(strip, pairs[2])
    strip_a = send(strip, pairs[3])
    side_a = send(specimen, pairs[0])

    inputs = (probe_modes, patterns, specimen, *dft_tables(n))
    probe_chip, _, own, *tables, power, root, measured = pl.pallas_call(
        prepare_kernel,
        out_shape=tuple(pltpu.VMEM(a.shape, a.dtype) for a in inputs)
        + (
            pltpu.VMEM((n, n), f32), pltpu.VMEM((count, n, n), f32), pltpu.VMEM((8, n), f32),
        ),
        in_specs=[pl.BlockSpec(memory_space=pltpu.HBM)] * 7,
        out_specs=tuple(vmem(10)),
        scratch_shapes=[pltpu.SemaphoreType.DMA((7,))],
        name="prepare",
        compiler_params=limit(8),
    )(*(pltpu.with_memory_space_constraint(a, pltpu.HBM) for a in inputs))

    wide = pltpu.VMEM((3, rows, cols), f32)
    narrow = pltpu.VMEM((3, rows, n), f32)
    planes = 2 * modes + 2
    ext_rows = rows + 2 * n + 8
    ext_cols = cols + 3 * n
    part = pltpu.VMEM((planes // PARTS, n // 2, n), f32)
    *halves, fold_own, fold_a, fold_b, fold_y, fold_ya, fold_yb = pl.pallas_call(
        positions_kernel,
        out_shape=(part,) * (2 * PARTS) + (wide, wide, wide, narrow, narrow, narrow),
        in_specs=[pl.BlockSpec(memory_space=pltpu.SMEM)] + vmem(14),
        out_specs=tuple(vmem(6 + 2 * PARTS)),
        scratch_shapes=[
            pltpu.VMEM((planes, n, n), f32),
            pltpu.VMEM((2, ext_rows, ext_cols), f32),
            pltpu.VMEM((3, ext_rows, ext_cols), f32),
            pltpu.VMEM((modes // 2, 2 * n, 2 * n), f32),
            pltpu.VMEM((2, n, n), f32),
            pltpu.VMEM((n, n), f32),
            pltpu.VMEM((2, n, n), f32),
        ],
        name="positions",
        compiler_params=limit(30),
    )(
        where,
        *on_chip(
            probe_chip, root, power, measured, own, side_a, side_b, strip_y, strip_a, strip_b,
            *tables,
        ),
    )

    keeps, sends = halves[0::2], halves[1::2]
    back_b = send(fold_b, pairs[1])
    back_yb = send(fold_yb, pairs[4])
    back_y = send(fold_y, pairs[2])
    back_ya = send(fold_ya, pairs[3])
    back_a = send(fold_a, pairs[0])

    new_probe = probe_update(where, probe_chip, keeps, sends, pairs[0], scan, tile)
    new_specimen = finish(where, own, fold_own, back_a, back_b, back_y, back_ya, back_yb)
    return (new_probe.reshape(probe_modes.shape), new_specimen)


def finish(where, own, *folds):
    return pl.pallas_call(
        object_kernel,
        out_shape=jax.ShapeDtypeStruct(own.shape, f32),
        in_specs=[pl.BlockSpec(memory_space=pltpu.SMEM)] + vmem(7),
        out_specs=vmem(1)[0],
        name="object",
        compiler_params=limit(4),
    )(where, *on_chip(own, *folds))


def solution(mesh):
    return jax.shard_map(
        program,
        mesh=mesh,
        in_specs=(
            P(),
            P(AXES, None, None),
            P(None, "scan", "tile"),
            P(AXES, None),
        ),
        out_specs=(P(), P(None, "scan", "tile")),
        check_vma=False,
    )
```

profile of v0, /device:TPU:21, one launch (start us, length us, event | category | flops | bytes accessed | tf_op | source)
XLA Modules:
  0.0 105.5 jit_solution(9014223373718190514)
XLA Ops:
  1.4 3.0 %collective-permute-start.1 = (f32[2,128,256]{2,1,0:T(8,128)}, f32[2,128,256]{2,1,0:T(8,128)S(1)}, u32[]{:S(2)}, u32[]{:S(2)}) collective-permute-start(f32[2,128,256]{2,1,0:T(8,128)} %refs_2_.1), channel_id=1, source_target_pairs={{2,4},{3,5},{4,2},{5,3},{6,8},{7,9},{8,6},{9,7},{10,12},{11,13},{1... | collective-permute-start | bytes 786440 | tf_op jit(solution)/shard_map/ppermute | solution.py:408
  4.4 0.9 constant_dynamic-slice_fusion
  5.3 2.5 %collective-permute-start.4 = (f32[2,128,128]{2,1,0:T(8,128)S(1)}, f32[2,128,128]{2,1,0:T(8,128)S(1)}, u32[]{:S(2)}, u32[]{:S(2)}) collective-permute-start(f32[2,128,128]{2,1,0:T(8,128)S(1)} %constant_dynamic-slice_fusion), channel_id=1, source_target_pairs={{2,5},{3,4},{4,3},{5,2},{6,9},{7,8},{8,7},{9,6},{10,13},{11,12},{1... | collective-permute-start | bytes 393224 | tf_op jit(solution)/shard_map/ppermute | solution.py:408
  7.8 2.1 %collective-permute-start.3 = (f32[2,128,128]{2,1,0:T(8,128)S(1)}, f32[2,128,128]{2,1,0:T(8,128)S(1)}, u32[]{:S(2)}, u32[]{:S(2)}) collective-permute-start(f32[2,128,128]{2,1,0:T(8,128)S(1)} %constant_dynamic-slice_fusion), channel_id=1, source_target_pairs={{0,3},{1,2},{2,1},{3,0},{4,7},{5,6},{6,5},{7,4},{8,11},{9,10},{10,... | collective-permute-start | bytes 393224 | tf_op jit(solution)/shard_map/ppermute | solution.py:408
  11.0 2.7 %prepare.1 = (f32[12,2,128,128]{3,2,1,0:T(8,128)S(1)}, f32[4,128,128]{2,1,0:T(8,128)}, f32[2,128,256]{2,1,0:T(8,128)S(1)}, bf16[768,256]{1,0:T(8,128)(2,1)S(1)},...) custom-call(f32[12,2,128,128]{3,2,1,0:T(8,128)} %refs_0_.1, ...), custom_call_target="tpu_custom_call" | custom-call | tf_op jit(solution)/shard_map/prepare/pallas_call | solution.py:496
  13.7 1.1 %collective-permute-done.4.strip_b = f32[2,128,128]{2,1,0:T(8,128)S(1)} collective-permute-done((f32[2,128,128]{2,1,0:T(8,128)S(1)}, f32[2,128,128]{2,1,0:T(8,128)S(1)}, u32[]{:S(2)}, u32[]{:S(2)}) %collective-permute-start.4) | collective-permute-done | bytes 131104 | tf_op jit(solution)/shard_map/ppermute | solution.py:408
  14.8 2.1 %collective-permute-done.3.strip_a = f32[2,128,128]{2,1,0:T(8,128)S(1)} collective-permute-done((f32[2,128,128]{2,1,0:T(8,128)S(1)}, f32[2,128,128]{2,1,0:T(8,128)S(1)}, u32[]{:S(2)}, u32[]{:S(2)}) %collective-permute-start.3) | collective-permute-done | bytes 131104 | tf_op jit(solution)/shard_map/ppermute | solution.py:408
  16.9 2.8 %collective-permute-done.2.strip_y = f32[2,128,128]{2,1,0:T(8,128)S(1)} collective-permute-done((f32[2,128,128]{2,1,0:T(8,128)S(1)}, f32[2,128,128]{2,1,0:T(8,128)S(1)}, u32[]{:S(2)}, u32[]{:S(2)}) %collective-permute-start.2) | collective-permute-done | bytes 131104 | tf_op jit(solution)/shard_map/ppermute | solution.py:408
  19.8 16.9 %positions.1 = (f32[13,64,128]{2,1,0:T(8,128)S(1)}, f32[13,64,128]{2,1,0:T(8,128)S(1)}, f32[13,64,128]{2,1,0:T(8,128)S(1)}, f32[13,64,128]{2,1,0:T(8,128)S(1)}, ...) custom-call(s32[11]{0:T(128)S(1)} %concatenate.3.where, ...), custom_call_target="tpu_custom_call" | custom-call | tf_op jit(solution)/shard_map/positions/pallas_call | solution.py:515
  37.3 1.3 %collective-permute-done.5.received = f32[13,64,128]{2,1,0:T(8,128)S(1)} collective-permute-done((f32[13,64,128]{2,1,0:T(8,128)S(1)}, f32[13,64,128]{2,1,0:T(8,128)S(1)}, u32[]{:S(2)}, u32[]{:S(2)}) %collective-permute-start.5) | collective-permute-done | bytes 426016 | tf_op jit(solution)/shard_map/ppermute | solution.py:408
  39.2 1.0 collective-permute-start.6
  40.8 1.1 %collective-permute-start.8 = (f32[13,16,128]{2,1,0:T(8,128)S(1)}, f32[13,16,128]{2,1,0:T(8,128)S(1)}, u32[]{:S(2)}, u32[]{:S(2)}) collective-permute-start(f32[13,16,128]{2,1,0:T(8,128)S(1)} %get-tuple-element.43), channel_id=1, source_target_pairs={{0,5},{1,4},{2,7},{3,6},{4,1},{5,0},{6,3},{7,2},{8,13},{9,12},{10,... | collective-permute-start | bytes 319496 | tf_op jit(solution)/shard_map/ppermute | solution.py:408
  42.5 1.0 collective-permute-start.16
  44.1 1.1 %collective-permute-start.18 = (f32[13,16,128]{2,1,0:T(8,128)S(1)}, f32[13,16,128]{2,1,0:T(8,128)S(1)}, u32[]{:S(2)}, u32[]{:S(2)}) collective-permute-start(f32[13,16,128]{2,1,0:T(8,128)S(1)} %get-tuple-element.49), channel_id=1, source_target_pairs={{0,5},{1,4},{2,7},{3,6},{4,1},{5,0},{6,3},{7,2},{8,13},{9,12},{10,... | collective-permute-start | bytes 319496 | tf_op jit(solution)/shard_map/ppermute | solution.py:408
  45.2 1.5 %collective-permute-done.8 = f32[13,16,128]{2,1,0:T(8,128)S(1)} collective-permute-done((f32[13,16,128]{2,1,0:T(8,128)S(1)}, f32[13,16,128]{2,1,0:T(8,128)S(1)}, u32[]{:S(2)}, u32[]{:S(2)}) %collective-permute-start.8) | collective-permute-done | bytes 106528 | tf_op jit(solution)/shard_map/ppermute | solution.py:408
  46.7 1.3 %collective-permute-start.9 = (f32[13,16,128]{2,1,0:T(8,128)S(1)}, f32[13,16,128]{2,1,0:T(8,128)S(1)}, u32[]{:S(2)}, u32[]{:S(2)}) collective-permute-start(f32[13,16,128]{2,1,0:T(8,128)S(1)} %add_add_fusion.1), channel_id=1, source_target_pairs={{0,8},{1,9},{2,10},{3,11},{4,12},{5,13},{6,14},{7,15},{8,0},{9,1},... | collective-permute-start | bytes 319496 | tf_op jit(solution)/shard_map/ppermute | solution.py:408
  48.8 2.5 %collective-permute-done.18 = f32[13,16,128]{2,1,0:T(8,128)S(1)} collective-permute-done((f32[13,16,128]{2,1,0:T(8,128)S(1)}, f32[13,16,128]{2,1,0:T(8,128)S(1)}, u32[]{:S(2)}, u32[]{:S(2)}) %collective-permute-start.18) | collective-permute-done | bytes 106528 | tf_op jit(solution)/shard_map/ppermute | solution.py:408
  51.3 1.3 %collective-permute-start.19 = (f32[13,16,128]{2,1,0:T(8,128)S(1)}, f32[13,16,128]{2,1,0:T(8,128)S(1)}, u32[]{:S(2)}, u32[]{:S(2)}) collective-permute-start(f32[13,16,128]{2,1,0:T(8,128)S(1)} %add_add_fusion), channel_id=1, source_target_pairs={{0,8},{1,9},{2,10},{3,11},{4,12},{5,13},{6,14},{7,15},{8,0},{9,1},... | collective-permute-start | bytes 319496 | tf_op jit(solution)/shard_map/ppermute | solution.py:408
  52.6 2.3 %collective-permute-done.19 = f32[13,16,128]{2,1,0:T(8,128)S(1)} collective-permute-done((f32[13,16,128]{2,1,0:T(8,128)S(1)}, f32[13,16,128]{2,1,0:T(8,128)S(1)}, u32[]{:S(2)}, u32[]{:S(2)}) %collective-permute-start.19) | collective-permute-done | bytes 106528 | tf_op jit(solution)/shard_map/ppermute | solution.py:408
  55.2 1.6 %collective-permute-done.10 = f32[13,16,128]{2,1,0:T(8,128)S(1)} collective-permute-done((f32[13,16,128]{2,1,0:T(8,128)S(1)}, f32[13,16,128]{2,1,0:T(8,128)S(1)}, u32[]{:S(2)}, u32[]{:S(2)}) %collective-permute-start.10) | collective-permute-done | bytes 106528 | tf_op jit(solution)/shard_map/ppermute | solution.py:408
  57.4 1.4 %collective-permute-start.12 = (f32[13,16,128]{2,1,0:T(8,128)S(1)}, f32[13,16,128]{2,1,0:T(8,128)S(1)}, u32[]{:S(2)}, u32[]{:S(2)}) collective-permute-start(f32[13,16,128]{2,1,0:T(8,128)S(1)} %add.54.refs_0_), channel_id=1, source_target_pairs={{0,4},{1,5},{2,6},{3,7},{4,0},{5,1},{6,2},{7,3},{8,12},{9,13},{10,... | collective-permute-start | bytes 319496 | tf_op jit(solution)/shard_map/ppermute | solution.py:408
  60.3 2.4 %collective-permute-done.20 = f32[13,16,128]{2,1,0:T(8,128)S(1)} collective-permute-done((f32[13,16,128]{2,1,0:T(8,128)S(1)}, f32[13,16,128]{2,1,0:T(8,128)S(1)}, u32[]{:S(2)}, u32[]{:S(2)}) %collective-permute-start.20) | collective-permute-done | bytes 106528 | tf_op jit(solution)/shard_map/ppermute | solution.py:408
  62.7 2.4 %collective-permute-start.23 = (f32[13,16,128]{2,1,0:T(8,128)S(1)}, f32[13,16,128]{2,1,0:T(8,128)S(1)}, u32[]{:S(2)}, u32[]{:S(2)}) collective-permute-start(f32[13,16,128]{2,1,0:T(8,128)S(1)} %add.59.refs_0_), channel_id=1, source_target_pairs={{0,5},{1,4},{2,7},{3,6},{4,1},{5,0},{6,3},{7,2},{8,13},{9,12},{10,... | collective-permute-start | bytes 319496 | tf_op jit(solution)/shard_map/ppermute | solution.py:408
  65.1 1.1 %collective-permute-start.21 = (f32[13,16,128]{2,1,0:T(8,128)S(1)}, f32[13,16,128]{2,1,0:T(8,128)S(1)}, u32[]{:S(2)}, u32[]{:S(2)}) collective-permute-start(f32[13,16,128]{2,1,0:T(8,128)S(1)} %add.59.refs_0_), channel_id=1, source_target_pairs={{0,1},{1,0},{2,3},{3,2},{4,5},{5,4},{6,7},{7,6},{8,9},{9,8},{10,11... | collective-permute-start | bytes 319496 | tf_op jit(solution)/shard_map/ppermute | solution.py:408
  66.7 8.5 %collective-permute-start.14 = (f32[13,64,128]{2,1,0:T(8,128)S(1)}, f32[13,64,128]{2,1,0:T(8,128)S(1)}, u32[]{:S(2)}, u32[]{:S(2)}) collective-permute-start(f32[13,64,128]{2,1,0:T(8,128)S(1)} %join.2.refs_0_), channel_id=1, source_target_pairs={{0,2},{1,3},{2,0},{3,1},{4,6},{5,7},{6,4},{7,5},{8,10},{9,11},{10,... | collective-permute-start | bytes 1277960 | tf_op jit(solution)/shard_map/ppermute | solution.py:408
  75.8 1.5 %collective-permute-start.24 = (f32[13,64,128]{2,1,0:T(8,128)S(1)}, f32[13,64,128]{2,1,0:T(8,128)S(1)}, u32[]{:S(2)}, u32[]{:S(2)}) collective-permute-start(f32[13,64,128]{2,1,0:T(8,128)S(1)} %join.3.refs_2_), channel_id=1, source_target_pairs={{0,2},{1,3},{2,0},{3,1},{4,6},{5,7},{6,4},{7,5},{8,10},{9,11},{10,... | collective-permute-start | bytes 1277960 | tf_op jit(solution)/shard_map/ppermute | solution.py:408
  77.7 3.6 %collective-permute-start.26 = (f32[3,128,256]{2,1,0:T(8,128)S(1)}, f32[3,128,256]{2,1,0:T(8,128)S(1)}, u32[]{:S(2)}, u32[]{:S(2)}) collective-permute-start(f32[3,128,256]{2,1,0:T(8,128)S(1)} %get-tuple-element.52), channel_id=1, source_target_pairs={{2,4},{3,5},{4,2},{5,3},{6,8},{7,9},{8,6},{9,7},{10,12},{11,13},{1... | collective-permute-start | bytes 1179656 | tf_op jit(solution)/shard_map/ppermute | solution.py:408
  81.3 2.9 %collective-permute-done.28.strip_a = f32[3,128,128]{2,1,0:T(8,128)S(1)} collective-permute-done((f32[3,128,128]{2,1,0:T(8,128)S(1)}, f32[3,128,128]{2,1,0:T(8,128)S(1)}, u32[]{:S(2)}, u32[]{:S(2)}) %collective-permute-start.28) | collective-permute-done | bytes 196640 | tf_op jit(solution)/shard_map/ppermute | solution.py:408
  84.2 3.0 %collective-permute-start.29 = (f32[3,128,128]{2,1,0:T(8,128)S(1)}, f32[3,128,128]{2,1,0:T(8,128)S(1)}, u32[]{:S(2)}, u32[]{:S(2)}) collective-permute-start(f32[3,128,128]{2,1,0:T(8,128)S(1)} %get-tuple-element.55), channel_id=1, source_target_pairs={{2,5},{3,4},{4,3},{5,2},{6,9},{7,8},{8,7},{9,6},{10,13},{11,12},{1... | collective-permute-start | bytes 589832 | tf_op jit(solution)/shard_map/ppermute | solution.py:408
  87.2 9.2 %collective-permute-done.29.strip_b = f32[3,128,128]{2,1,0:T(8,128)S(1)} collective-permute-done((f32[3,128,128]{2,1,0:T(8,128)S(1)}, f32[3,128,128]{2,1,0:T(8,128)S(1)}, u32[]{:S(2)}, u32[]{:S(2)}) %collective-permute-start.29) | collective-permute-done | bytes 196640 | tf_op jit(solution)/shard_map/ppermute | solution.py:408
  96.4 1.4 %object.1 = f32[2,128,256]{2,1,0:T(8,128)} custom-call(s32[11]{0:T(128)S(1)} %concatenate.3.where, f32[2,128,256]{2,1,0:T(8,128)S(1)} %get-tuple-element.33.own.specimen, f32[3,128,256]{2,1,0:T(8,128)S(1)} %get-tuple-element.50.own, f32[3,128,256]{2,1,0:T(8,128)S(1)} %collective-permute-done.25.side_a, f32[3,128,256]{2,1,0:T(8,128)S(1)} %collective-permute-done.26.side_b, ...), custom_call_target="tpu_custom_call" | custom-call | tf_op jit(solution)/shard_map/object/pallas_call | solution.py:552
  97.8 7.7 %probe.1 = f32[24,128,128]{2,1,0:T(8,128)} custom-call(s32[11]{0:T(128)S(1)} %concatenate.3.where, f32[12,2,128,128]{3,2,1,0:T(8,128)S(1)} %get-tuple-element.29.probe, f32[13,64,128]{2,1,0:T(8,128)S(1)} %join.2.refs_0_, f32[13,64,128]{2,1,0:T(8,128)S(1)} %collective-permute-done.14.refs_1_, f32[13,64,128]{2,1,0:T(8,128)S(1)} %join.3.refs_2_, ...), custom_call_target="tpu_custom_call" | custom-call | tf_op jit(solution)/shard_map/probe/pallas_call | solution.py:454
  (45 shorter events, 9.9 us)
Async XLA Ops:
  0.6 19.1 %collective-permute-start = (f32[2,128,256]{2,1,0:T(8,128)}, f32[2,128,256]{2,1,0:T(8,128)S(1)}, u32[]{:S(2)}, u32[]{:S(2)}) collective-permute-start(f32[2,128,256]{2,1,0:T(8,128)} %refs_2_.1), channel_id=1, source_target_pairs={{0,2},{1,3},{2,0},{3,1},{4,6},{5,7},{6,4},{7,5},{8,10},{9,11},{10,... | collective-permute-start | bytes 786440 | tf_op jit(solution)/shard_map/ppermute | solution.py:408
  1.4 18.4 %collective-permute-start.1 = (f32[2,128,256]{2,1,0:T(8,128)}, f32[2,128,256]{2,1,0:T(8,128)S(1)}, u32[]{:S(2)}, u32[]{:S(2)}) collective-permute-start(f32[2,128,256]{2,1,0:T(8,128)} %refs_2_.1), channel_id=1, source_target_pairs={{2,4},{3,5},{4,2},{5,3},{6,8},{7,9},{8,6},{9,7},{10,12},{11,13},{1... | collective-permute-start | bytes 786440 | tf_op jit(solution)/shard_map/ppermute | solution.py:408
  5.3 9.5 %collective-permute-start.4 = (f32[2,128,128]{2,1,0:T(8,128)S(1)}, f32[2,128,128]{2,1,0:T(8,128)S(1)}, u32[]{:S(2)}, u32[]{:S(2)}) collective-permute-start(f32[2,128,128]{2,1,0:T(8,128)S(1)} %constant_dynamic-slice_fusion), channel_id=1, source_target_pairs={{2,5},{3,4},{4,3},{5,2},{6,9},{7,8},{8,7},{9,6},{10,13},{11,12},{1... | collective-permute-start | bytes 393224 | tf_op jit(solution)/shard_map/ppermute | solution.py:408
  7.8 9.1 %collective-permute-start.3 = (f32[2,128,128]{2,1,0:T(8,128)S(1)}, f32[2,128,128]{2,1,0:T(8,128)S(1)}, u32[]{:S(2)}, u32[]{:S(2)}) collective-permute-start(f32[2,128,128]{2,1,0:T(8,128)S(1)} %constant_dynamic-slice_fusion), channel_id=1, source_target_pairs={{0,3},{1,2},{2,1},{3,0},{4,7},{5,6},{6,5},{7,4},{8,11},{9,10},{10,... | collective-permute-start | bytes 393224 | tf_op jit(solution)/shard_map/ppermute | solution.py:408
  9.9 9.8 %collective-permute-start.2 = (f32[2,128,128]{2,1,0:T(8,128)S(1)}, f32[2,128,128]{2,1,0:T(8,128)S(1)}, u32[]{:S(2)}, u32[]{:S(2)}) collective-permute-start(f32[2,128,128]{2,1,0:T(8,128)S(1)} %constant_dynamic-slice_fusion), channel_id=1, source_target_pairs={{0,1},{1,0},{2,3},{3,2},{4,5},{5,4},{6,7},{7,6},{8,9},{9,8},{10,11... | collective-permute-start | bytes 393224 | tf_op jit(solution)/shard_map/ppermute | solution.py:408
  36.6 1.9 %collective-permute-start.5 = (f32[13,64,128]{2,1,0:T(8,128)S(1)}, f32[13,64,128]{2,1,0:T(8,128)S(1)}, u32[]{:S(2)}, u32[]{:S(2)}) collective-permute-start(f32[13,64,128]{2,1,0:T(8,128)S(1)} %get-tuple-element.39), channel_id=1, source_target_pairs={{0,2},{1,3},{2,0},{3,1},{4,6},{5,7},{6,4},{7,5},{8,10},{9,11},{10,... | collective-permute-start | bytes 1277960 | tf_op jit(solution)/shard_map/ppermute | solution.py:408
  37.2 4.7 %collective-permute-start.15 = (f32[13,64,128]{2,1,0:T(8,128)S(1)}, f32[13,64,128]{2,1,0:T(8,128)S(1)}, u32[]{:S(2)}, u32[]{:S(2)}) collective-permute-start(f32[13,64,128]{2,1,0:T(8,128)S(1)} %get-tuple-element.45), channel_id=1, source_target_pairs={{0,2},{1,3},{2,0},{3,1},{4,6},{5,7},{6,4},{7,5},{8,10},{9,11},{10,... | collective-permute-start | bytes 1277960 | tf_op jit(solution)/shard_map/ppermute | solution.py:408
  39.2 4.9 %collective-permute-start.6 = (f32[13,16,128]{2,1,0:T(8,128)S(1)}, f32[13,16,128]{2,1,0:T(8,128)S(1)}, u32[]{:S(2)}, u32[]{:S(2)}) collective-permute-start(f32[13,16,128]{2,1,0:T(8,128)S(1)} %get-tuple-element.41), channel_id=1, source_target_pairs={{0,1},{1,0},{2,3},{3,2},{4,5},{5,4},{6,7},{7,6},{8,9},{9,8},{10,11... | collective-permute-start | bytes 319496 | tf_op jit(solution)/shard_map/ppermute | solution.py:408
  40.1 5.1 %collective-permute-start.7 = (f32[13,16,128]{2,1,0:T(8,128)S(1)}, f32[13,16,128]{2,1,0:T(8,128)S(1)}, u32[]{:S(2)}, u32[]{:S(2)}) collective-permute-start(f32[13,16,128]{2,1,0:T(8,128)S(1)} %get-tuple-element.42), channel_id=1, source_target_pairs={{0,4},{1,5},{2,6},{3,7},{4,0},{5,1},{6,2},{7,3},{8,12},{9,13},{10,... | collective-permute-start | bytes 319496 | tf_op jit(solution)/shard_map/ppermute | solution.py:408
  40.8 5.9 %collective-permute-start.8 = (f32[13,16,128]{2,1,0:T(8,128)S(1)}, f32[13,16,128]{2,1,0:T(8,128)S(1)}, u32[]{:S(2)}, u32[]{:S(2)}) collective-permute-start(f32[13,16,128]{2,1,0:T(8,128)S(1)} %get-tuple-element.43), channel_id=1, source_target_pairs={{0,5},{1,4},{2,7},{3,6},{4,1},{5,0},{6,3},{7,2},{8,13},{9,12},{10,... | collective-permute-start | bytes 319496 | tf_op jit(solution)/shard_map/ppermute | solution.py:408
  42.5 6.1 %collective-permute-start.16 = (f32[13,16,128]{2,1,0:T(8,128)S(1)}, f32[13,16,128]{2,1,0:T(8,128)S(1)}, u32[]{:S(2)}, u32[]{:S(2)}) collective-permute-start(f32[13,16,128]{2,1,0:T(8,128)S(1)} %get-tuple-element.47), channel_id=1, source_target_pairs={{0,1},{1,0},{2,3},{3,2},{4,5},{5,4},{6,7},{7,6},{8,9},{9,8},{10,11... | collective-permute-start | bytes 319496 | tf_op jit(solution)/shard_map/ppermute | solution.py:408
  43.5 5.3 %collective-permute-start.17 = (f32[13,16,128]{2,1,0:T(8,128)S(1)}, f32[13,16,128]{2,1,0:T(8,128)S(1)}, u32[]{:S(2)}, u32[]{:S(2)}) collective-permute-start(f32[13,16,128]{2,1,0:T(8,128)S(1)} %get-tuple-element.48), channel_id=1, source_target_pairs={{0,4},{1,5},{2,6},{3,7},{4,0},{5,1},{6,2},{7,3},{8,12},{9,13},{10,... | collective-permute-start | bytes 319496 | tf_op jit(solution)/shard_map/ppermute | solution.py:408
  44.1 7.1 %collective-permute-start.18 = (f32[13,16,128]{2,1,0:T(8,128)S(1)}, f32[13,16,128]{2,1,0:T(8,128)S(1)}, u32[]{:S(2)}, u32[]{:S(2)}) collective-permute-start(f32[13,16,128]{2,1,0:T(8,128)S(1)} %get-tuple-element.49), channel_id=1, source_target_pairs={{0,5},{1,4},{2,7},{3,6},{4,1},{5,0},{6,3},{7,2},{8,13},{9,12},{10,... | collective-permute-start | bytes 319496 | tf_op jit(solution)/shard_map/ppermute | solution.py:408
  46.7 5.8 %collective-permute-start.9 = (f32[13,16,128]{2,1,0:T(8,128)S(1)}, f32[13,16,128]{2,1,0:T(8,128)S(1)}, u32[]{:S(2)}, u32[]{:S(2)}) collective-permute-start(f32[13,16,128]{2,1,0:T(8,128)S(1)} %add_add_fusion.1), channel_id=1, source_target_pairs={{0,8},{1,9},{2,10},{3,11},{4,12},{5,13},{6,14},{7,15},{8,0},{9,1},... | collective-permute-start | bytes 319496 | tf_op jit(solution)/shard_map/ppermute | solution.py:408
  51.3 3.6 %collective-permute-start.19 = (f32[13,16,128]{2,1,0:T(8,128)S(1)}, f32[13,16,128]{2,1,0:T(8,128)S(1)}, u32[]{:S(2)}, u32[]{:S(2)}) collective-permute-start(f32[13,16,128]{2,1,0:T(8,128)S(1)} %add_add_fusion), channel_id=1, source_target_pairs={{0,8},{1,9},{2,10},{3,11},{4,12},{5,13},{6,14},{7,15},{8,0},{9,1},... | collective-permute-start | bytes 319496 | tf_op jit(solution)/shard_map/ppermute | solution.py:408
  52.6 4.2 %collective-permute-start.10 = (f32[13,16,128]{2,1,0:T(8,128)S(1)}, f32[13,16,128]{2,1,0:T(8,128)S(1)}, u32[]{:S(2)}, u32[]{:S(2)}) collective-permute-start(f32[13,16,128]{2,1,0:T(8,128)S(1)} %add.53), channel_id=1, source_target_pairs={{0,24},{1,25},{2,26},{3,27},{4,28},{5,29},{6,30},{7,31},{8,16},{9,... | collective-permute-start | bytes 319496 | tf_op jit(solution)/shard_map/ppermute | solution.py:408
  54.9 7.7 %collective-permute-start.20 = (f32[13,16,128]{2,1,0:T(8,128)S(1)}, f32[13,16,128]{2,1,0:T(8,128)S(1)}, u32[]{:S(2)}, u32[]{:S(2)}) collective-permute-start(f32[13,16,128]{2,1,0:T(8,128)S(1)} %add.58), channel_id=1, source_target_pairs={{0,24},{1,25},{2,26},{3,27},{4,28},{5,29},{6,30},{7,31},{8,16},{9,... | collective-permute-start | bytes 319496 | tf_op jit(solution)/shard_map/ppermute | solution.py:408
  56.7 8.3 %collective-permute-start.13 = (f32[13,16,128]{2,1,0:T(8,128)S(1)}, f32[13,16,128]{2,1,0:T(8,128)S(1)}, u32[]{:S(2)}, u32[]{:S(2)}) collective-permute-start(f32[13,16,128]{2,1,0:T(8,128)S(1)} %add.54.refs_0_), channel_id=1, source_target_pairs={{0,5},{1,4},{2,7},{3,6},{4,1},{5,0},{6,3},{7,2},{8,13},{9,12},{10,... | collective-permute-start | bytes 319496 | tf_op jit(solution)/shard_map/ppermute | solution.py:408
  57.4 7.6 %collective-permute-start.12 = (f32[13,16,128]{2,1,0:T(8,128)S(1)}, f32[13,16,128]{2,1,0:T(8,128)S(1)}, u32[]{:S(2)}, u32[]{:S(2)}) collective-permute-start(f32[13,16,128]{2,1,0:T(8,128)S(1)} %add.54.refs_0_), channel_id=1, source_target_pairs={{0,4},{1,5},{2,6},{3,7},{4,0},{5,1},{6,2},{7,3},{8,12},{9,13},{10,... | collective-permute-start | bytes 319496 | tf_op jit(solution)/shard_map/ppermute | solution.py:408
  58.8 18.9 %collective-permute-start.27 = (f32[3,128,128]{2,1,0:T(8,128)S(1)}, f32[3,128,128]{2,1,0:T(8,128)S(1)}, u32[]{:S(2)}, u32[]{:S(2)}) collective-permute-start(f32[3,128,128]{2,1,0:T(8,128)S(1)} %get-tuple-element.53), channel_id=1, source_target_pairs={{0,1},{1,0},{2,3},{3,2},{4,5},{5,4},{6,7},{7,6},{8,9},{9,8},{10,11... | collective-permute-start | bytes 589832 | tf_op jit(solution)/shard_map/ppermute | solution.py:408
  59.5 6.7 %collective-permute-start.11 = (f32[13,16,128]{2,1,0:T(8,128)S(1)}, f32[13,16,128]{2,1,0:T(8,128)S(1)}, u32[]{:S(2)}, u32[]{:S(2)}) collective-permute-start(f32[13,16,128]{2,1,0:T(8,128)S(1)} %add.54.refs_0_), channel_id=1, source_target_pairs={{0,1},{1,0},{2,3},{3,2},{4,5},{5,4},{6,7},{7,6},{8,9},{9,8},{10,11... | collective-permute-start | bytes 319496 | tf_op jit(solution)/shard_map/ppermute | solution.py:408
  62.7 12.5 %collective-permute-start.23 = (f32[13,16,128]{2,1,0:T(8,128)S(1)}, f32[13,16,128]{2,1,0:T(8,128)S(1)}, u32[]{:S(2)}, u32[]{:S(2)}) collective-permute-start(f32[13,16,128]{2,1,0:T(8,128)S(1)} %add.59.refs_0_), channel_id=1, source_target_pairs={{0,5},{1,4},{2,7},{3,6},{4,1},{5,0},{6,3},{7,2},{8,13},{9,12},{10,... | collective-permute-start | bytes 319496 | tf_op jit(solution)/shard_map/ppermute | solution.py:408
  65.0 10.2 %collective-permute-start.22 = (f32[13,16,128]{2,1,0:T(8,128)S(1)}, f32[13,16,128]{2,1,0:T(8,128)S(1)}, u32[]{:S(2)}, u32[]{:S(2)}) collective-permute-start(f32[13,16,128]{2,1,0:T(8,128)S(1)} %add.59.refs_0_), channel_id=1, source_target_pairs={{0,4},{1,5},{2,6},{3,7},{4,0},{5,1},{6,2},{7,3},{8,12},{9,13},{10,... | collective-permute-start | bytes 319496 | tf_op jit(solution)/shard_map/ppermute | solution.py:408
  65.1 10.2 %collective-permute-start.21 = (f32[13,16,128]{2,1,0:T(8,128)S(1)}, f32[13,16,128]{2,1,0:T(8,128)S(1)}, u32[]{:S(2)}, u32[]{:S(2)}) collective-permute-start(f32[13,16,128]{2,1,0:T(8,128)S(1)} %add.59.refs_0_), channel_id=1, source_target_pairs={{0,1},{1,0},{2,3},{3,2},{4,5},{5,4},{6,7},{7,6},{8,9},{9,8},{10,11... | collective-permute-start | bytes 319496 | tf_op jit(solution)/shard_map/ppermute | solution.py:408
  66.7 31.1 %collective-permute-start.14 = (f32[13,64,128]{2,1,0:T(8,128)S(1)}, f32[13,64,128]{2,1,0:T(8,128)S(1)}, u32[]{:S(2)}, u32[]{:S(2)}) collective-permute-start(f32[13,64,128]{2,1,0:T(8,128)S(1)} %join.2.refs_0_), channel_id=1, source_target_pairs={{0,2},{1,3},{2,0},{3,1},{4,6},{5,7},{6,4},{7,5},{8,10},{9,11},{10,... | collective-permute-start | bytes 1277960 | tf_op jit(solution)/shard_map/ppermute | solution.py:408
  75.8 22.0 %collective-permute-start.24 = (f32[13,64,128]{2,1,0:T(8,128)S(1)}, f32[13,64,128]{2,1,0:T(8,128)S(1)}, u32[]{:S(2)}, u32[]{:S(2)}) collective-permute-start(f32[13,64,128]{2,1,0:T(8,128)S(1)} %join.3.refs_2_), channel_id=1, source_target_pairs={{0,2},{1,3},{2,0},{3,1},{4,6},{5,7},{6,4},{7,5},{8,10},{9,11},{10,... | collective-permute-start | bytes 1277960 | tf_op jit(solution)/shard_map/ppermute | solution.py:408
  77.3 6.9 %collective-permute-start.28 = (f32[3,128,128]{2,1,0:T(8,128)S(1)}, f32[3,128,128]{2,1,0:T(8,128)S(1)}, u32[]{:S(2)}, u32[]{:S(2)}) collective-permute-start(f32[3,128,128]{2,1,0:T(8,128)S(1)} %get-tuple-element.54), channel_id=1, source_target_pairs={{0,3},{1,2},{2,1},{3,0},{4,7},{5,6},{6,5},{7,4},{8,11},{9,10},{10,... | collective-permute-start | bytes 589832 | tf_op jit(solution)/shard_map/ppermute | solution.py:408
  77.3 19.1 %collective-permute-start.25 = (f32[3,128,256]{2,1,0:T(8,128)S(1)}, f32[3,128,256]{2,1,0:T(8,128)S(1)}, u32[]{:S(2)}, u32[]{:S(2)}) collective-permute-start(f32[3,128,256]{2,1,0:T(8,128)S(1)} %get-tuple-element.51), channel_id=1, source_target_pairs={{0,2},{1,3},{2,0},{3,1},{4,6},{5,7},{6,4},{7,5},{8,10},{9,11},{10,... | collective-permute-start | bytes 1179656 | tf_op jit(solution)/shard_map/ppermute | solution.py:408
  77.7 18.7 %collective-permute-start.26 = (f32[3,128,256]{2,1,0:T(8,128)S(1)}, f32[3,128,256]{2,1,0:T(8,128)S(1)}, u32[]{:S(2)}, u32[]{:S(2)}) collective-permute-start(f32[3,128,256]{2,1,0:T(8,128)S(1)} %get-tuple-element.52), channel_id=1, source_target_pairs={{2,4},{3,5},{4,2},{5,3},{6,8},{7,9},{8,6},{9,7},{10,12},{11,13},{1... | collective-permute-start | bytes 1179656 | tf_op jit(solution)/shard_map/ppermute | solution.py:408
  84.2 12.2 %collective-permute-start.29 = (f32[3,128,128]{2,1,0:T(8,128)S(1)}, f32[3,128,128]{2,1,0:T(8,128)S(1)}, u32[]{:S(2)}, u32[]{:S(2)}) collective-permute-start(f32[3,128,128]{2,1,0:T(8,128)S(1)} %get-tuple-element.55), channel_id=1, source_target_pairs={{2,5},{3,4},{4,3},{5,2},{6,9},{7,8},{8,7},{9,6},{10,13},{11,12},{1... | collective-permute-start | bytes 589832 | tf_op jit(solution)/shard_map/ppermute | solution.py:408
where the time goes:
time: 106 us
  starting transfers between devices  41.4 us (39%)
  Pallas kernels  31.1 us (29%)
  waiting for transfers between devices  30.3 us (29%)
    ppermute x30, starting transfers between devices, send(): return lax.ppermute(array, AXES, pairs)  41.4 us
    ppermute x30, waiting for transfers between devices, send(): return lax.ppermute(array, AXES, pairs)  30.3 us
    pallas_call x1, Pallas kernels, program(): pl.pallas_call(positions_kernel, out_shape=(part,) * (2 * PARTS) + (wide,...  16.9 us
    pallas_call x1, Pallas kernels, probe_update(): pl.pallas_call(probe_kernel, out_shape=jax.ShapeDtypeStruct((planes, n, n...  7.67 us
    pallas_call x1, Pallas kernels, program(): pl.pallas_call(prepare_kernel, out_shape=tuple((pltpu.VMEM(a.shape, a.dty...  2.74 us
  transfers between devices with their start and end apart: 30, of which 13 were waited for; matrix products, arithmetic and copies ran while one was open for 2% of the time, Pallas kernels for 6%

commit v1 on v0

--- a/solution.py
+++ b/solution.py
@@ -94,8 +94,8 @@
     *refs,
 ):
     parts = refs[: 2 * PARTS]
-    fold_own, fold_a, fold_b, fold_y, fold_ya, fold_yb = refs[2 * PARTS : 2 * PARTS + 6]
-    sums, extended, frame, far, patch, model, numer = refs[2 * PARTS + 6 :]
+    fold_own, fold_a, fold_b, fold_y = refs[2 * PARTS : 2 * PARTS + 4]
+    sums, extended, frame, far, patch, model, numer = refs[2 * PARTS + 4 :]
     modes, _, n, _ = probe.shape
     count = root.shape[0]
     rows, cols = own.shape[1:]
@@ -202,25 +202,31 @@
     fold_own[...] = frame[:, n : n + rows, n : n + cols]
     fold_a[...] = frame[:, pl.ds(row_a, n), n : n + cols]
     fold_b[...] = frame[:, pl.ds(row_b, n), n : n + cols]
-    fold_y[...] = frame[:, n : n + rows, pl.ds(col_y, n)]
-    fold_ya[...] = frame[:, pl.ds(row_a, n), pl.ds(col_y, n)]
-    fold_yb[...] = frame[:, pl.ds(row_b, n), pl.ds(col_y, n)]
+    fold_y[0] = frame[:, n : n + rows, pl.ds(col_y, n)]
+    fold_y[1] = frame[:, pl.ds(row_a, n), pl.ds(col_y, n)]
+    fold_y[2] = frame[:, pl.ds(row_b, n), pl.ds(col_y, n)]
 
 
 UNROLL = 6
 PARTS = 2
 
 
-def object_kernel(where, specimen, own, side_a, side_b, strip_y, strip_a, strip_b, out):
-    n = strip_y.shape[2]
-    cols = own.shape[2]
+def edge_kernel(where, column, *refs):
+    n = column.shape[3]
+    cols = refs[0].shape[2]
     first_tile = where[where.shape[0] - 2] == 0
     at = pl.multiple_of(jnp.where(first_tile, cols - n, 0), n)
-    own[...] += side_a[...] + side_b[...]
-    own[:, :, pl.ds(at, n)] += strip_y[...] + strip_a[...] + strip_b[...]
-    light = own[2] + object_reg
-    out[0] = specimen[0] + own[0] / light
-    out[1] = specimen[1] + own[1] / light
+    for k in range(3):
+        out = refs[3 + k]
+        out[...] = refs[k][...]
+        out[:, :, pl.ds(at, n)] += column[k]
+
+
+def object_kernel(specimen, own, side_a, side_b, after, out):
+    total = own[...] + side_a[...] + side_b[...]
+    light = total[2] + object_reg
+    out[0] = specimen[0] + total[0] / light
+    out[1] = specimen[1] + total[1] / light
 
 
 def split_kernel(where, keep, received, *outs):
@@ -337,7 +343,9 @@
         factor = 1.5 * identity - 0.5 * mul(inverse, current)
         return mul(current, factor), mul(factor, inverse)
 
-    _, inverse = lax.fori_loop(0, NS_STEPS, newton, (hermitian / frobenius, identity))
+    current = hermitian / frobenius
+    factor = 1.5 * identity - 0.5 * current
+    _, inverse = lax.fori_loop(1, NS_STEPS, newton, (mul(current, factor), factor))
     inverse = inverse / jnp.sqrt(frobenius)
     diagonal = jnp.sum(hermitian * identity, axis=1, keepdims=True)
     mix = inverse * jnp.sqrt(ratio * diagonal)
@@ -507,16 +515,16 @@
     )(*(pltpu.with_memory_space_constraint(a, pltpu.HBM) for a in inputs))
 
     wide = pltpu.VMEM((3, rows, cols), f32)
-    narrow = pltpu.VMEM((3, rows, n), f32)
+    column = pltpu.VMEM((3, 3, rows, n), f32)
     planes = 2 * modes + 2
     ext_rows = rows + 2 * n + 8
     ext_cols = cols + 3 * n
     part = pltpu.VMEM((planes // PARTS, n // 2, n), f32)
-    *halves, fold_own, fold_a, fold_b, fold_y, fold_ya, fold_yb = pl.pallas_call(
+    *halves, fold_own, fold_a, fold_b, fold_y = pl.pallas_call(
         positions_kernel,
-        out_shape=(part,) * (2 * PARTS) + (wide, wide, wide, narrow, narrow, narrow),
+        out_shape=(part,) * (2 * PARTS) + (wide, wide, wide, column),
         in_specs=[pl.BlockSpec(memory_space=pltpu.SMEM)] + vmem(14),
-        out_specs=tuple(vmem(6 + 2 * PARTS)),
+        out_specs=tuple(vmem(4 + 2 * PARTS)),
         scratch_shapes=[
             pltpu.VMEM((planes, n, n), f32),
             pltpu.VMEM((2, ext_rows, ext_cols), f32),
@@ -537,26 +545,32 @@
     )
 
     keeps, sends = halves[0::2], halves[1::2]
+    back_y = send(fold_y, pairs[2])
+    fold_own, fold_a, fold_b = pl.pallas_call(
+        edge_kernel,
+        out_shape=(wide,) * 3,
+        in_specs=[pl.BlockSpec(memory_space=pltpu.SMEM)] + vmem(4),
+        out_specs=tuple(vmem(3)),
+        name="edges",
+        compiler_params=limit(6),
+    )(where, *on_chip(back_y, fold_own, fold_a, fold_b))
     back_b = send(fold_b, pairs[1])
-    back_yb = send(fold_yb, pairs[4])
-    back_y = send(fold_y, pairs[2])
-    back_ya = send(fold_ya, pairs[3])
     back_a = send(fold_a, pairs[0])
 
     new_probe = probe_update(where, probe_chip, keeps, sends, pairs[0], scan, tile)
-    new_specimen = finish(where, own, fold_own, back_a, back_b, back_y, back_ya, back_yb)
+    new_specimen = finish(new_probe, own, fold_own, back_a, back_b)
     return (new_probe.reshape(probe_modes.shape), new_specimen)
 
 
-def finish(where, own, *folds):
+def finish(after, own, *folds):
     return pl.pallas_call(
         object_kernel,
         out_shape=jax.ShapeDtypeStruct(own.shape, f32),
-        in_specs=[pl.BlockSpec(memory_space=pltpu.SMEM)] + vmem(7),
+        in_specs=vmem(4) + [pl.BlockSpec(memory_space=pltpu.HBM)],
         out_specs=vmem(1)[0],
         name="object",
         compiler_params=limit(4),
-    )(where, *on_chip(own, *folds))
+    )(*on_chip(own, *folds), pltpu.with_memory_space_constraint(after, pltpu.HBM))
 
 
 def solution(mesh):

time: 106 us -> 104 us (0.981)
  the two profiles are of different devices: /device:TPU:21 before, /device:TPU:9 now
where the time goes in v1:
time: 104 us
  starting transfers between devices  38.3 us (37%)
  waiting for transfers between devices  32 us (31%)
  Pallas kernels  30.9 us (30%)
    ppermute x28, starting transfers between devices, send(): return lax.ppermute(array, AXES, pairs)  38.3 us
    ppermute x28, waiting for transfers between devices, send(): return lax.ppermute(array, AXES, pairs)  32 us
    pallas_call x1, Pallas kernels, program(): pl.pallas_call(positions_kernel, out_shape=(part,) * (2 * PARTS) + (wide,...  16.9 us
    pallas_call x1, Pallas kernels, probe_update(): pl.pallas_call(probe_kernel, out_shape=jax.ShapeDtypeStruct((planes, n, n...  7.42 us
    pallas_call x1, Pallas kernels, program(): pl.pallas_call(prepare_kernel, out_shape=tuple((pltpu.VMEM(a.shape, a.dty...  2.74 us
  transfers between devices with their start and end apart: 28, of which 9 were waited for; matrix products, arithmetic and copies ran while one was open for 2% of the time, Pallas kernels for 13%

profile of v1, /device:TPU:9, one launch (start us, length us, event | category | flops | bytes accessed | tf_op | source)
XLA Modules:
  0.0 103.9 jit_solution(7520706729253310766)
XLA Ops:
  1.4 3.0 %collective-permute-start.1 = (f32[2,128,256]{2,1,0:T(8,128)}, f32[2,128,256]{2,1,0:T(8,128)S(1)}, u32[]{:S(2)}, u32[]{:S(2)}) collective-permute-start(f32[2,128,256]{2,1,0:T(8,128)} %refs_2_.1), channel_id=1, source_target_pairs={{2,4},{3,5},{4,2},{5,3},{6,8},{7,9},{8,6},{9,7},{10,12},{11,13},{1... | collective-permute-start | bytes 786440 | tf_op jit(solution)/shard_map/ppermute | solution.py:416
  4.4 0.9 constant_dynamic-slice_fusion
  5.3 3.5 %collective-permute-start.4 = (f32[2,128,128]{2,1,0:T(8,128)S(1)}, f32[2,128,128]{2,1,0:T(8,128)S(1)}, u32[]{:S(2)}, u32[]{:S(2)}) collective-permute-start(f32[2,128,128]{2,1,0:T(8,128)S(1)} %constant_dynamic-slice_fusion), channel_id=1, source_target_pairs={{2,5},{3,4},{4,3},{5,2},{6,9},{7,8},{8,7},{9,6},{10,13},{11,12},{1... | collective-permute-start | bytes 393224 | tf_op jit(solution)/shard_map/ppermute | solution.py:416
  8.8 1.1 %collective-permute-start.3 = (f32[2,128,128]{2,1,0:T(8,128)S(1)}, f32[2,128,128]{2,1,0:T(8,128)S(1)}, u32[]{:S(2)}, u32[]{:S(2)}) collective-permute-start(f32[2,128,128]{2,1,0:T(8,128)S(1)} %constant_dynamic-slice_fusion), channel_id=1, source_target_pairs={{0,3},{1,2},{2,1},{3,0},{4,7},{5,6},{6,5},{7,4},{8,11},{9,10},{10,... | collective-permute-start | bytes 393224 | tf_op jit(solution)/shard_map/ppermute | solution.py:416
  9.9 1.2 %collective-permute-start.2 = (f32[2,128,128]{2,1,0:T(8,128)S(1)}, f32[2,128,128]{2,1,0:T(8,128)S(1)}, u32[]{:S(2)}, u32[]{:S(2)}) collective-permute-start(f32[2,128,128]{2,1,0:T(8,128)S(1)} %constant_dynamic-slice_fusion), channel_id=1, source_target_pairs={{0,1},{1,0},{2,3},{3,2},{4,5},{5,4},{6,7},{7,6},{8,9},{9,8},{10,11... | collective-permute-start | bytes 393224 | tf_op jit(solution)/shard_map/ppermute | solution.py:416
  11.2 0.8 subtract_bitcast_fusion
  12.0 2.7 %prepare.1 = (f32[12,2,128,128]{3,2,1,0:T(8,128)S(1)}, f32[4,128,128]{2,1,0:T(8,128)}, f32[2,128,256]{2,1,0:T(8,128)S(1)}, bf16[768,256]{1,0:T(8,128)(2,1)S(1)},...) custom-call(f32[12,2,128,128]{3,2,1,0:T(8,128)} %refs_0_.1, ...), custom_call_target="tpu_custom_call" | custom-call | tf_op jit(solution)/shard_map/prepare/pallas_call | solution.py:504
  14.8 1.2 %collective-permute-done.4.strip_b = f32[2,128,128]{2,1,0:T(8,128)S(1)} collective-permute-done((f32[2,128,128]{2,1,0:T(8,128)S(1)}, f32[2,128,128]{2,1,0:T(8,128)S(1)}, u32[]{:S(2)}, u32[]{:S(2)}) %collective-permute-start.4) | collective-permute-done | bytes 131104 | tf_op jit(solution)/shard_map/ppermute | solution.py:416
  15.9 1.7 %collective-permute-done.3.strip_a = f32[2,128,128]{2,1,0:T(8,128)S(1)} collective-permute-done((f32[2,128,128]{2,1,0:T(8,128)S(1)}, f32[2,128,128]{2,1,0:T(8,128)S(1)}, u32[]{:S(2)}, u32[]{:S(2)}) %collective-permute-start.3) | collective-permute-done | bytes 131104 | tf_op jit(solution)/shard_map/ppermute | solution.py:416
  17.7 2.8 %collective-permute-done.2.strip_y = f32[2,128,128]{2,1,0:T(8,128)S(1)} collective-permute-done((f32[2,128,128]{2,1,0:T(8,128)S(1)}, f32[2,128,128]{2,1,0:T(8,128)S(1)}, u32[]{:S(2)}, u32[]{:S(2)}) %collective-permute-start.2) | collective-permute-done | bytes 131104 | tf_op jit(solution)/shard_map/ppermute | solution.py:416
  20.5 16.9 %positions.1 = (f32[13,64,128]{2,1,0:T(8,128)S(1)}, f32[13,64,128]{2,1,0:T(8,128)S(1)}, f32[13,64,128]{2,1,0:T(8,128)S(1)}, f32[13,64,128]{2,1,0:T(8,128)S(1)}, ...) custom-call(s32[11]{0:T(128)S(1)} %concatenate.3.where, ...), custom_call_target="tpu_custom_call" | custom-call | tf_op jit(solution)/shard_map/positions/pallas_call | solution.py:523
  38.0 1.3 %collective-permute-done.5.received = f32[13,64,128]{2,1,0:T(8,128)S(1)} collective-permute-done((f32[13,64,128]{2,1,0:T(8,128)S(1)}, f32[13,64,128]{2,1,0:T(8,128)S(1)}, u32[]{:S(2)}, u32[]{:S(2)}) %collective-permute-start.5) | collective-permute-done | bytes 426016 | tf_op jit(solution)/shard_map/ppermute | solution.py:416
  40.5 1.1 %collective-permute-start.7 = (f32[13,16,128]{2,1,0:T(8,128)S(1)}, f32[13,16,128]{2,1,0:T(8,128)S(1)}, u32[]{:S(2)}, u32[]{:S(2)}) collective-permute-start(f32[13,16,128]{2,1,0:T(8,128)S(1)} %get-tuple-element.43), channel_id=1, source_target_pairs={{0,4},{1,5},{2,6},{3,7},{4,0},{5,1},{6,2},{7,3},{8,12},{9,13},{10,... | collective-permute-start | bytes 319496 | tf_op jit(solution)/shard_map/ppermute | solution.py:416
  41.6 1.0 collective-permute-start.8
  43.7 1.0 collective-permute-start.16
  45.4 1.1 %collective-permute-start.18 = (f32[13,16,128]{2,1,0:T(8,128)S(1)}, f32[13,16,128]{2,1,0:T(8,128)S(1)}, u32[]{:S(2)}, u32[]{:S(2)}) collective-permute-start(f32[13,16,128]{2,1,0:T(8,128)S(1)} %get-tuple-element.50), channel_id=1, source_target_pairs={{0,5},{1,4},{2,7},{3,6},{4,1},{5,0},{6,3},{7,2},{8,13},{9,12},{10,... | collective-permute-start | bytes 319496 | tf_op jit(solution)/shard_map/ppermute | solution.py:416
  46.5 1.0 collective-permute-done.8
  47.6 16.3 %collective-permute-done.16 = f32[13,16,128]{2,1,0:T(8,128)S(1)} collective-permute-done((f32[13,16,128]{2,1,0:T(8,128)S(1)}, f32[13,16,128]{2,1,0:T(8,128)S(1)}, u32[]{:S(2)}, u32[]{:S(2)}) %collective-permute-start.16) | collective-permute-done | bytes 106528 | tf_op jit(solution)/shard_map/ppermute | solution.py:416
  64.0 2.5 %collective-permute-start.10 = (f32[13,16,128]{2,1,0:T(8,128)S(1)}, f32[13,16,128]{2,1,0:T(8,128)S(1)}, u32[]{:S(2)}, u32[]{:S(2)}) collective-permute-start(f32[13,16,128]{2,1,0:T(8,128)S(1)} %add.53), channel_id=1, source_target_pairs={{0,24},{1,25},{2,26},{3,27},{4,28},{5,29},{6,30},{7,31},{8,16},{9,... | collective-permute-start | bytes 319496 | tf_op jit(solution)/shard_map/ppermute | solution.py:416
  66.6 1.0 collective-permute-done.19
  67.5 1.4 %collective-permute-start.20 = (f32[13,16,128]{2,1,0:T(8,128)S(1)}, f32[13,16,128]{2,1,0:T(8,128)S(1)}, u32[]{:S(2)}, u32[]{:S(2)}) collective-permute-start(f32[13,16,128]{2,1,0:T(8,128)S(1)} %add.58), channel_id=1, source_target_pairs={{0,24},{1,25},{2,26},{3,27},{4,28},{5,29},{6,30},{7,31},{8,16},{9,... | collective-permute-start | bytes 319496 | tf_op jit(solution)/shard_map/ppermute | solution.py:416
  69.0 1.3 %collective-permute-start.13 = (f32[13,16,128]{2,1,0:T(8,128)S(1)}, f32[13,16,128]{2,1,0:T(8,128)S(1)}, u32[]{:S(2)}, u32[]{:S(2)}) collective-permute-start(f32[13,16,128]{2,1,0:T(8,128)S(1)} %add.54.refs_0_), channel_id=1, source_target_pairs={{0,5},{1,4},{2,7},{3,6},{4,1},{5,0},{6,3},{7,2},{8,13},{9,12},{10,... | collective-permute-start | bytes 319496 | tf_op jit(solution)/shard_map/ppermute | solution.py:416
  70.3 1.3 %collective-permute-start.12 = (f32[13,16,128]{2,1,0:T(8,128)S(1)}, f32[13,16,128]{2,1,0:T(8,128)S(1)}, u32[]{:S(2)}, u32[]{:S(2)}) collective-permute-start(f32[13,16,128]{2,1,0:T(8,128)S(1)} %add.54.refs_0_), channel_id=1, source_target_pairs={{0,4},{1,5},{2,6},{3,7},{4,0},{5,1},{6,2},{7,3},{8,12},{9,13},{10,... | collective-permute-start | bytes 319496 | tf_op jit(solution)/shard_map/ppermute | solution.py:416
  71.7 4.5 %collective-permute-done.20 = f32[13,16,128]{2,1,0:T(8,128)S(1)} collective-permute-done((f32[13,16,128]{2,1,0:T(8,128)S(1)}, f32[13,16,128]{2,1,0:T(8,128)S(1)}, u32[]{:S(2)}, u32[]{:S(2)}) %collective-permute-start.20) | collective-permute-done | bytes 106528 | tf_op jit(solution)/shard_map/ppermute | solution.py:416
  76.2 1.3 %collective-permute-start.23 = (f32[13,16,128]{2,1,0:T(8,128)S(1)}, f32[13,16,128]{2,1,0:T(8,128)S(1)}, u32[]{:S(2)}, u32[]{:S(2)}) collective-permute-start(f32[13,16,128]{2,1,0:T(8,128)S(1)} %add.59.refs_0_), channel_id=1, source_target_pairs={{0,5},{1,4},{2,7},{3,6},{4,1},{5,0},{6,3},{7,2},{8,13},{9,12},{10,... | collective-permute-start | bytes 319496 | tf_op jit(solution)/shard_map/ppermute | solution.py:416
  78.0 0.9 collective-permute-start.21
  79.5 5.8 %collective-permute-start.14 = (f32[13,64,128]{2,1,0:T(8,128)S(1)}, f32[13,64,128]{2,1,0:T(8,128)S(1)}, u32[]{:S(2)}, u32[]{:S(2)}) collective-permute-start(f32[13,64,128]{2,1,0:T(8,128)S(1)} %join.2.refs_0_), channel_id=1, source_target_pairs={{0,2},{1,3},{2,0},{3,1},{4,6},{5,7},{6,4},{7,5},{8,10},{9,11},{10,... | collective-permute-start | bytes 1277960 | tf_op jit(solution)/shard_map/ppermute | solution.py:416
  85.8 2.8 %collective-permute-start.24 = (f32[13,64,128]{2,1,0:T(8,128)S(1)}, f32[13,64,128]{2,1,0:T(8,128)S(1)}, u32[]{:S(2)}, u32[]{:S(2)}) collective-permute-start(f32[13,64,128]{2,1,0:T(8,128)S(1)} %join.3.refs_2_), channel_id=1, source_target_pairs={{0,2},{1,3},{2,0},{3,1},{4,6},{5,7},{6,4},{7,5},{8,10},{9,11},{10,... | collective-permute-start | bytes 1277960 | tf_op jit(solution)/shard_map/ppermute | solution.py:416
  89.4 4.0 %collective-permute-start.27 = (f32[3,128,256]{2,1,0:T(8,128)S(1)}, f32[3,128,256]{2,1,0:T(8,128)S(1)}, u32[]{:S(2)}, u32[]{:S(2)}) collective-permute-start(f32[3,128,256]{2,1,0:T(8,128)S(1)} %get-tuple-element.57), channel_id=1, source_target_pairs={{2,4},{3,5},{4,2},{5,3},{6,8},{7,9},{8,6},{9,7},{10,12},{11,13},{1... | collective-permute-start | bytes 1179656 | tf_op jit(solution)/shard_map/ppermute | solution.py:416
  93.5 7.4 %probe.1.after = f32[24,128,128]{2,1,0:T(8,128)} custom-call(s32[11]{0:T(128)S(1)} %concatenate.3.where, f32[12,2,128,128]{3,2,1,0:T(8,128)S(1)} %get-tuple-element.30.probe, f32[13,64,128]{2,1,0:T(8,128)S(1)} %join.2.refs_0_, f32[13,64,128]{2,1,0:T(8,128)S(1)} %collective-permute-done.14.refs_1_, f32[13,64,128]{2,1,0:T(8,128)S(1)} %join.3.refs_2_, ...), custom_call_target="tpu_custom_call" | custom-call | tf_op jit(solution)/shard_map/probe/pallas_call | solution.py:462
  100.9 2.2 %collective-permute-done.27.side_b = f32[3,128,256]{2,1,0:T(8,128)S(1)} collective-permute-done((f32[3,128,256]{2,1,0:T(8,128)S(1)}, f32[3,128,256]{2,1,0:T(8,128)S(1)}, u32[]{:S(2)}, u32[]{:S(2)}) %collective-permute-start.27) | collective-permute-done | bytes 393248 | tf_op jit(solution)/shard_map/ppermute | solution.py:416
  103.1 0.8 object.1
  (42 shorter events, 7.4 us)
Async XLA Ops:
  0.6 19.9 %collective-permute-start = (f32[2,128,256]{2,1,0:T(8,128)}, f32[2,128,256]{2,1,0:T(8,128)S(1)}, u32[]{:S(2)}, u32[]{:S(2)}) collective-permute-start(f32[2,128,256]{2,1,0:T(8,128)} %refs_2_.1), channel_id=1, source_target_pairs={{0,2},{1,3},{2,0},{3,1},{4,6},{5,7},{6,4},{7,5},{8,10},{9,11},{10,... | collective-permute-start | bytes 786440 | tf_op jit(solution)/shard_map/ppermute | solution.py:416
  1.4 19.1 %collective-permute-start.1 = (f32[2,128,256]{2,1,0:T(8,128)}, f32[2,128,256]{2,1,0:T(8,128)S(1)}, u32[]{:S(2)}, u32[]{:S(2)}) collective-permute-start(f32[2,128,256]{2,1,0:T(8,128)} %refs_2_.1), channel_id=1, source_target_pairs={{2,4},{3,5},{4,2},{5,3},{6,8},{7,9},{8,6},{9,7},{10,12},{11,13},{1... | collective-permute-start | bytes 786440 | tf_op jit(solution)/shard_map/ppermute | solution.py:416
  5.3 10.6 %collective-permute-start.4 = (f32[2,128,128]{2,1,0:T(8,128)S(1)}, f32[2,128,128]{2,1,0:T(8,128)S(1)}, u32[]{:S(2)}, u32[]{:S(2)}) collective-permute-start(f32[2,128,128]{2,1,0:T(8,128)S(1)} %constant_dynamic-slice_fusion), channel_id=1, source_target_pairs={{2,5},{3,4},{4,3},{5,2},{6,9},{7,8},{8,7},{9,6},{10,13},{11,12},{1... | collective-permute-start | bytes 393224 | tf_op jit(solution)/shard_map/ppermute | solution.py:416
  8.8 8.9 %collective-permute-start.3 = (f32[2,128,128]{2,1,0:T(8,128)S(1)}, f32[2,128,128]{2,1,0:T(8,128)S(1)}, u32[]{:S(2)}, u32[]{:S(2)}) collective-permute-start(f32[2,128,128]{2,1,0:T(8,128)S(1)} %constant_dynamic-slice_fusion), channel_id=1, source_target_pairs={{0,3},{1,2},{2,1},{3,0},{4,7},{5,6},{6,5},{7,4},{8,11},{9,10},{10,... | collective-permute-start | bytes 393224 | tf_op jit(solution)/shard_map/ppermute | solution.py:416
  9.9 10.6 %collective-permute-start.2 = (f32[2,128,128]{2,1,0:T(8,128)S(1)}, f32[2,128,128]{2,1,0:T(8,128)S(1)}, u32[]{:S(2)}, u32[]{:S(2)}) collective-permute-start(f32[2,128,128]{2,1,0:T(8,128)S(1)} %constant_dynamic-slice_fusion), channel_id=1, source_target_pairs={{0,1},{1,0},{2,3},{3,2},{4,5},{5,4},{6,7},{7,6},{8,9},{9,8},{10,11... | collective-permute-start | bytes 393224 | tf_op jit(solution)/shard_map/ppermute | solution.py:416
  37.4 1.9 %collective-permute-start.5 = (f32[13,64,128]{2,1,0:T(8,128)S(1)}, f32[13,64,128]{2,1,0:T(8,128)S(1)}, u32[]{:S(2)}, u32[]{:S(2)}) collective-permute-start(f32[13,64,128]{2,1,0:T(8,128)S(1)} %get-tuple-element.40), channel_id=1, source_target_pairs={{0,2},{1,3},{2,0},{3,1},{4,6},{5,7},{6,4},{7,5},{8,10},{9,11},{10,... | collective-permute-start | bytes 1277960 | tf_op jit(solution)/shard_map/ppermute | solution.py:416
  37.8 5.3 %collective-permute-start.15 = (f32[13,64,128]{2,1,0:T(8,128)S(1)}, f32[13,64,128]{2,1,0:T(8,128)S(1)}, u32[]{:S(2)}, u32[]{:S(2)}) collective-permute-start(f32[13,64,128]{2,1,0:T(8,128)S(1)} %get-tuple-element.46), channel_id=1, source_target_pairs={{0,2},{1,3},{2,0},{3,1},{4,6},{5,7},{6,4},{7,5},{8,10},{9,11},{10,... | collective-permute-start | bytes 1277960 | tf_op jit(solution)/shard_map/ppermute | solution.py:416
  39.8 4.9 %collective-permute-start.6 = (f32[13,16,128]{2,1,0:T(8,128)S(1)}, f32[13,16,128]{2,1,0:T(8,128)S(1)}, u32[]{:S(2)}, u32[]{:S(2)}) collective-permute-start(f32[13,16,128]{2,1,0:T(8,128)S(1)} %get-tuple-element.42), channel_id=1, source_target_pairs={{0,1},{1,0},{2,3},{3,2},{4,5},{5,4},{6,7},{7,6},{8,9},{9,8},{10,11... | collective-permute-start | bytes 319496 | tf_op jit(solution)/shard_map/ppermute | solution.py:416
  40.5 4.9 %collective-permute-start.7 = (f32[13,16,128]{2,1,0:T(8,128)S(1)}, f32[13,16,128]{2,1,0:T(8,128)S(1)}, u32[]{:S(2)}, u32[]{:S(2)}) collective-permute-start(f32[13,16,128]{2,1,0:T(8,128)S(1)} %get-tuple-element.43), channel_id=1, source_target_pairs={{0,4},{1,5},{2,6},{3,7},{4,0},{5,1},{6,2},{7,3},{8,12},{9,13},{10,... | collective-permute-start | bytes 319496 | tf_op jit(solution)/shard_map/ppermute | solution.py:416
  41.6 5.9 %collective-permute-start.8 = (f32[13,16,128]{2,1,0:T(8,128)S(1)}, f32[13,16,128]{2,1,0:T(8,128)S(1)}, u32[]{:S(2)}, u32[]{:S(2)}) collective-permute-start(f32[13,16,128]{2,1,0:T(8,128)S(1)} %get-tuple-element.44), channel_id=1, source_target_pairs={{0,5},{1,4},{2,7},{3,6},{4,1},{5,0},{6,3},{7,2},{8,13},{9,12},{10,... | collective-permute-start | bytes 319496 | tf_op jit(solution)/shard_map/ppermute | solution.py:416
  42.6 46.1 %collective-permute-start.25 = (f32[3,3,128,128]{3,2,1,0:T(8,128)S(1)}, f32[3,3,128,128]{3,2,1,0:T(8,128)S(1)}, u32[]{:S(2)}, u32[]{:S(2)}) collective-permute-start(f32[3,3,128,128]{3,2,1,0:T(8,128)S(1)} %get-tuple-element.51), channel_id=1, source_target_pairs={{0,1},{1,0},{2,3},{3,2},{4,5},{5,4},{6,7},{7,6},{8,9},{9,8},{10,11... | collective-permute-start | bytes 1769480 | tf_op jit(solution)/shard_map/ppermute | solution.py:416
  43.7 20.1 %collective-permute-start.16 = (f32[13,16,128]{2,1,0:T(8,128)S(1)}, f32[13,16,128]{2,1,0:T(8,128)S(1)}, u32[]{:S(2)}, u32[]{:S(2)}) collective-permute-start(f32[13,16,128]{2,1,0:T(8,128)S(1)} %get-tuple-element.48), channel_id=1, source_target_pairs={{0,1},{1,0},{2,3},{3,2},{4,5},{5,4},{6,7},{7,6},{8,9},{9,8},{10,11... | collective-permute-start | bytes 319496 | tf_op jit(solution)/shard_map/ppermute | solution.py:416
  44.7 19.2 %collective-permute-start.17 = (f32[13,16,128]{2,1,0:T(8,128)S(1)}, f32[13,16,128]{2,1,0:T(8,128)S(1)}, u32[]{:S(2)}, u32[]{:S(2)}) collective-permute-start(f32[13,16,128]{2,1,0:T(8,128)S(1)} %get-tuple-element.49), channel_id=1, source_target_pairs={{0,4},{1,5},{2,6},{3,7},{4,0},{5,1},{6,2},{7,3},{8,12},{9,13},{10,... | collective-permute-start | bytes 319496 | tf_op jit(solution)/shard_map/ppermute | solution.py:416
  45.4 18.5 %collective-permute-start.18 = (f32[13,16,128]{2,1,0:T(8,128)S(1)}, f32[13,16,128]{2,1,0:T(8,128)S(1)}, u32[]{:S(2)}, u32[]{:S(2)}) collective-permute-start(f32[13,16,128]{2,1,0:T(8,128)S(1)} %get-tuple-element.50), channel_id=1, source_target_pairs={{0,5},{1,4},{2,7},{3,6},{4,1},{5,0},{6,3},{7,2},{8,13},{9,12},{10,... | collective-permute-start | bytes 319496 | tf_op jit(solution)/shard_map/ppermute | solution.py:416
  47.5 16.5 %collective-permute-start.9 = (f32[13,16,128]{2,1,0:T(8,128)S(1)}, f32[13,16,128]{2,1,0:T(8,128)S(1)}, u32[]{:S(2)}, u32[]{:S(2)}) collective-permute-start(f32[13,16,128]{2,1,0:T(8,128)S(1)} %add_add_fusion.1), channel_id=1, source_target_pairs={{0,8},{1,9},{2,10},{3,11},{4,12},{5,13},{6,14},{7,15},{8,0},{9,1},... | collective-permute-start | bytes 319496 | tf_op jit(solution)/shard_map/ppermute | solution.py:416
  63.9 3.6 %collective-permute-start.19 = (f32[13,16,128]{2,1,0:T(8,128)S(1)}, f32[13,16,128]{2,1,0:T(8,128)S(1)}, u32[]{:S(2)}, u32[]{:S(2)}) collective-permute-start(f32[13,16,128]{2,1,0:T(8,128)S(1)} %add_add_fusion), channel_id=1, source_target_pairs={{0,8},{1,9},{2,10},{3,11},{4,12},{5,13},{6,14},{7,15},{8,0},{9,1},... | collective-permute-start | bytes 319496 | tf_op jit(solution)/shard_map/ppermute | solution.py:416
  64.0 4.9 %collective-permute-start.10 = (f32[13,16,128]{2,1,0:T(8,128)S(1)}, f32[13,16,128]{2,1,0:T(8,128)S(1)}, u32[]{:S(2)}, u32[]{:S(2)}) collective-permute-start(f32[13,16,128]{2,1,0:T(8,128)S(1)} %add.53), channel_id=1, source_target_pairs={{0,24},{1,25},{2,26},{3,27},{4,28},{5,29},{6,30},{7,31},{8,16},{9,... | collective-permute-start | bytes 319496 | tf_op jit(solution)/shard_map/ppermute | solution.py:416
  67.5 8.6 %collective-permute-start.20 = (f32[13,16,128]{2,1,0:T(8,128)S(1)}, f32[13,16,128]{2,1,0:T(8,128)S(1)}, u32[]{:S(2)}, u32[]{:S(2)}) collective-permute-start(f32[13,16,128]{2,1,0:T(8,128)S(1)} %add.58), channel_id=1, source_target_pairs={{0,24},{1,25},{2,26},{3,27},{4,28},{5,29},{6,30},{7,31},{8,16},{9,... | collective-permute-start | bytes 319496 | tf_op jit(solution)/shard_map/ppermute | solution.py:416
  69.0 8.5 %collective-permute-start.13 = (f32[13,16,128]{2,1,0:T(8,128)S(1)}, f32[13,16,128]{2,1,0:T(8,128)S(1)}, u32[]{:S(2)}, u32[]{:S(2)}) collective-permute-start(f32[13,16,128]{2,1,0:T(8,128)S(1)} %add.54.refs_0_), channel_id=1, source_target_pairs={{0,5},{1,4},{2,7},{3,6},{4,1},{5,0},{6,3},{7,2},{8,13},{9,12},{10,... | collective-permute-start | bytes 319496 | tf_op jit(solution)/shard_map/ppermute | solution.py:416
  70.3 7.7 %collective-permute-start.12 = (f32[13,16,128]{2,1,0:T(8,128)S(1)}, f32[13,16,128]{2,1,0:T(8,128)S(1)}, u32[]{:S(2)}, u32[]{:S(2)}) collective-permute-start(f32[13,16,128]{2,1,0:T(8,128)S(1)} %add.54.refs_0_), channel_id=1, source_target_pairs={{0,4},{1,5},{2,6},{3,7},{4,0},{5,1},{6,2},{7,3},{8,12},{9,13},{10,... | collective-permute-start | bytes 319496 | tf_op jit(solution)/shard_map/ppermute | solution.py:416
  71.5 7.4 %collective-permute-start.11 = (f32[13,16,128]{2,1,0:T(8,128)S(1)}, f32[13,16,128]{2,1,0:T(8,128)S(1)}, u32[]{:S(2)}, u32[]{:S(2)}) collective-permute-start(f32[13,16,128]{2,1,0:T(8,128)S(1)} %add.54.refs_0_), channel_id=1, source_target_pairs={{0,1},{1,0},{2,3},{3,2},{4,5},{5,4},{6,7},{7,6},{8,9},{9,8},{10,11... | collective-permute-start | bytes 319496 | tf_op jit(solution)/shard_map/ppermute | solution.py:416
  76.2 9.1 %collective-permute-start.23 = (f32[13,16,128]{2,1,0:T(8,128)S(1)}, f32[13,16,128]{2,1,0:T(8,128)S(1)}, u32[]{:S(2)}, u32[]{:S(2)}) collective-permute-start(f32[13,16,128]{2,1,0:T(8,128)S(1)} %add.59.refs_0_), channel_id=1, source_target_pairs={{0,5},{1,4},{2,7},{3,6},{4,1},{5,0},{6,3},{7,2},{8,13},{9,12},{10,... | collective-permute-start | bytes 319496 | tf_op jit(solution)/shard_map/ppermute | solution.py:416
  77.5 7.7 %collective-permute-start.22 = (f32[13,16,128]{2,1,0:T(8,128)S(1)}, f32[13,16,128]{2,1,0:T(8,128)S(1)}, u32[]{:S(2)}, u32[]{:S(2)}) collective-permute-start(f32[13,16,128]{2,1,0:T(8,128)S(1)} %add.59.refs_0_), channel_id=1, source_target_pairs={{0,4},{1,5},{2,6},{3,7},{4,0},{5,1},{6,2},{7,3},{8,12},{9,13},{10,... | collective-permute-start | bytes 319496 | tf_op jit(solution)/shard_map/ppermute | solution.py:416
  78.0 7.3 %collective-permute-start.21 = (f32[13,16,128]{2,1,0:T(8,128)S(1)}, f32[13,16,128]{2,1,0:T(8,128)S(1)}, u32[]{:S(2)}, u32[]{:S(2)}) collective-permute-start(f32[13,16,128]{2,1,0:T(8,128)S(1)} %add.59.refs_0_), channel_id=1, source_target_pairs={{0,1},{1,0},{2,3},{3,2},{4,5},{5,4},{6,7},{7,6},{8,9},{9,8},{10,11... | collective-permute-start | bytes 319496 | tf_op jit(solution)/shard_map/ppermute | solution.py:416
  79.5 14.0 %collective-permute-start.14 = (f32[13,64,128]{2,1,0:T(8,128)S(1)}, f32[13,64,128]{2,1,0:T(8,128)S(1)}, u32[]{:S(2)}, u32[]{:S(2)}) collective-permute-start(f32[13,64,128]{2,1,0:T(8,128)S(1)} %join.2.refs_0_), channel_id=1, source_target_pairs={{0,2},{1,3},{2,0},{3,1},{4,6},{5,7},{6,4},{7,5},{8,10},{9,11},{10,... | collective-permute-start | bytes 1277960 | tf_op jit(solution)/shard_map/ppermute | solution.py:416
  85.8 7.6 %collective-permute-start.24 = (f32[13,64,128]{2,1,0:T(8,128)S(1)}, f32[13,64,128]{2,1,0:T(8,128)S(1)}, u32[]{:S(2)}, u32[]{:S(2)}) collective-permute-start(f32[13,64,128]{2,1,0:T(8,128)S(1)} %join.3.refs_2_), channel_id=1, source_target_pairs={{0,2},{1,3},{2,0},{3,1},{4,6},{5,7},{6,4},{7,5},{8,10},{9,11},{10,... | collective-permute-start | bytes 1277960 | tf_op jit(solution)/shard_map/ppermute | solution.py:416
  89.4 11.5 %collective-permute-start.26 = (f32[3,128,256]{2,1,0:T(8,128)S(1)}, f32[3,128,256]{2,1,0:T(8,128)S(1)}, u32[]{:S(2)}, u32[]{:S(2)}) collective-permute-start(f32[3,128,256]{2,1,0:T(8,128)S(1)} %get-tuple-element.56), channel_id=1, source_target_pairs={{0,2},{1,3},{2,0},{3,1},{4,6},{5,7},{6,4},{7,5},{8,10},{9,11},{10,... | collective-permute-start | bytes 1179656 | tf_op jit(solution)/shard_map/ppermute | solution.py:416
  89.4 13.7 %collective-permute-start.27 = (f32[3,128,256]{2,1,0:T(8,128)S(1)}, f32[3,128,256]{2,1,0:T(8,128)S(1)}, u32[]{:S(2)}, u32[]{:S(2)}) collective-permute-start(f32[3,128,256]{2,1,0:T(8,128)S(1)} %get-tuple-element.57), channel_id=1, source_target_pairs={{2,4},{3,5},{4,2},{5,3},{6,8},{7,9},{8,6},{9,7},{10,12},{11,13},{1... | collective-permute-start | bytes 1179656 | tf_op jit(solution)/shard_map/ppermute | solution.py:416
